TPU v7x, 512 devices: a whole 4x4x16 slice. The times are simulated.
512 devices in a mesh: section: 16 (over x_lo, y, core), shard: 32 (over z, x_hi).
Axes of the slice: x: 4 (x_hi: 2, x_lo: 2; x = x_hi * 2 + x_lo), y: 4, z: 16, core: 2. Of those that a mesh axis runs over, the one named last changes fastest.
Arguments:
- train_weights: float32 [16, 16384, 1024], P('section', 'shard'), may hold values from -0.046875 to 0.046875
- section_to_group: int32 [16], replicated, may hold values from 0 to 15, each once
- hidden: bfloat16 [2048, 16384], P(('section', 'shard')), may hold values from -6 to 6
- queries: bfloat16 [8192, 2048], P(('section', 'shard')), may hold values from -100 to 100
- kv_cache: bfloat16 [8192, 128, 256], P(('section', 'shard')), may hold values from -5 to 5
- lengths: int32 [2048], P('section'), may hold values from 2 to 127, as said below
Outputs:
- context: bfloat16 [8192, 2048], P(('section', 'shard'))
- layer_out: bfloat16 [16, 4, 256, 16384], P('section', None, 'shard')
Inputs may be any that keep to these rules, and one draw needn't show every extreme that they name: `section_to_group`: a permutation: each rollout group runs exactly one trainer section's layer. `lengths`: every row has at least two cached tokens; some row of every device has 127.
All inputs are finite; a program needn't handle non-finite values.
Results may differ from a plain program's by a relative error of at most 0.006.
Values may be sent and summed in bfloat16 or wider, within the bound.
No kernel may reach another device: no remote copies, remote signals or barrier semaphores. Data moves between devices by JAX's collectives and lax.ppermute only.
A program may use at most 64 MiB of HBM per device.

v0:
```python
import math

import jax
import jax.numpy as jnp
from jax import lax
from jax.experimental import pallas as pl
from jax.experimental.pallas import tpu as pltpu
from jax.sharding import PartitionSpec as P


D = 16384
HD = 128
QPK = 16
KVH = 4
LEN = 128
ROWS = 128
ROW_TILE = 128


def exchange(blocks, axis):
    return lax.all_to_all(blocks, axis, split_axis=0, concat_axis=0, tiled=True)


def spread_rows(keep, other):
    shards = lax.axis_size("shard")

    def send(values, bits):
        return lax.ppermute(values, "shard", [(i, i ^ bits) for i in range(shards)])

    side = [keep, send(other, 1)]
    near = [jnp.stack([v[k] for v in side]) for k in range(4)]
    near = [near[0]] + [send(near[k], k << 1) for k in range(1, 4)]
    far = [jnp.stack([v[:, k] for v in near]) for k in range(4)]
    for k in (2, 1, 3):
        far[k] = send(far[k], k << 3)
    return jnp.concatenate(far).reshape((shards,) + keep.shape[2:])


def attend(query_rows, cache_rows, fresh_rows, row_lengths):
    score_scale = 1.0 / math.sqrt(HD)
    cached_keys = cache_rows[:, :, :HD]
    cached_values = cache_rows[:, :, HD:]
    key_new = fresh_rows[:, :HD]
    value_new = fresh_rows[:, HD:]
    scores = (
        jnp.einsum("rhd,rtd->rht", query_rows, cached_keys, preferred_element_type=jnp.float32)
        * score_scale
    )
    valid = jnp.arange(LEN)[None, None, :] < row_lengths[:, None, None]
    scores = jnp.where(valid, scores, -1e30)
    fresh_score = (
        jnp.einsum("rhd,rd->rh", query_rows, key_new, preferred_element_type=jnp.float32)
        * score_scale
    )
    highest = jnp.maximum(jnp.max(scores, axis=-1), fresh_score)
    weights = jnp.where(valid, jnp.exp(scores - highest[..., None]), 0.0)
    fresh_weight = jnp.exp(fresh_score - highest)
    total = jnp.sum(weights, axis=-1) + fresh_weight
    probs = (weights / total[..., None]).astype(jnp.bfloat16)
    fresh_prob = (fresh_weight / total).astype(jnp.bfloat16)
    context = jnp.einsum("rht,rtd->rhd", probs, cached_values, preferred_element_type=jnp.float32)
    context = (
        context
        + fresh_prob.astype(jnp.float32)[..., None] * value_new.astype(jnp.float32)[:, None, :]
    )
    return context.reshape(context.shape[0], QPK * HD).astype(jnp.bfloat16)


VMEM = pl.BlockSpec(memory_space=pltpu.VMEM)


def enter_kernel(
    me_ref, weights_ref, hidden_ref, out_ref, keep_ref, send_ref,
    weights_buf, out_buf, hidden_buf, in_sems, out_sems, hidden_sem,
):
    steps, rows, _ = weights_buf.shape
    _, shards, piece, width = out_buf.shape
    columns = shards * piece
    me = me_ref[0]
    hidden_copy = pltpu.make_async_copy(hidden_ref, hidden_buf, hidden_sem)
    hidden_copy.start()
    reads = [
        pltpu.make_async_copy(
            weights_ref.at[0, i * rows : (i + 1) * rows], weights_buf.at[i], in_sems.at[i]
        )
        for i in range(steps)
    ]
    for read in reads:
        read.start()
    hidden_copy.wait()
    depth = steps * rows
    for low in range(4):
        for high in range(4):
            for x, ref in ((0, keep_ref), (1, send_ref)):
                start = (me ^ (high * 8 + low * 2 + x)) * depth
                ref[low, high] = hidden_buf[:, pl.ds(pl.multiple_of(start, depth), depth)]
    writes = []
    for i in range(steps):
        reads[i].wait()
        for h in range(KVH):
            block = weights_buf[i, :, h * columns : (h + 1) * columns].astype(jnp.bfloat16)
            out_buf[i, :, :, h * rows : (h + 1) * rows] = block.T.reshape(shards, piece, rows)
        write = pltpu.make_async_copy(
            out_buf.at[i], out_ref.at[:, :, i * width : (i + 1) * width], out_sems.at[i]
        )
        write.start()
        writes.append(write)
    for write in writes:
        write.wait()


def enter(me, weights, hidden, shards):
    _, depth, columns = weights.shape
    piece = columns // KVH // shards
    steps = depth // ROW_TILE
    hbm = pl.BlockSpec(memory_space=pltpu.HBM)
    blocks = jax.ShapeDtypeStruct((4, 4, hidden.shape[0], depth), hidden.dtype)
    return pl.pallas_call(
        enter_kernel,
        in_specs=[pl.BlockSpec(memory_space=pltpu.SMEM), hbm, hbm],
        out_specs=[hbm, VMEM, VMEM],
        out_shape=[
            jax.ShapeDtypeStruct((shards, piece, KVH * depth), jnp.bfloat16), blocks, blocks
        ],
        scratch_shapes=[
            pltpu.VMEM((steps, ROW_TILE, columns), jnp.float32),
            pltpu.VMEM((steps, shards, piece, KVH * ROW_TILE), jnp.bfloat16),
            pltpu.VMEM(hidden.shape, hidden.dtype),
            pltpu.SemaphoreType.DMA((steps,)),
            pltpu.SemaphoreType.DMA((steps,)),
            pltpu.SemaphoreType.DMA,
        ],
        compiler_params=pltpu.CompilerParams(vmem_limit_bytes=63 * 1024 * 1024),
        cost_estimate=pl.CostEstimate(flops=2_000_000, bytes_accessed=3_000_000, transcendentals=0),
        name="enter",
    )(me, weights, hidden)


def pick_kernel(group_ref, spread_ref, out_ref):
    def move(s, carry):
        out_ref[group_ref[s]] = spread_ref[s]
        return carry

    lax.fori_loop(0, spread_ref.shape[0], move, 0)


def pick(section_to_group, spread):
    return pl.pallas_call(
        pick_kernel,
        in_specs=[pl.BlockSpec(memory_space=pltpu.SMEM), VMEM],
        out_specs=VMEM,
        out_shape=jax.ShapeDtypeStruct(spread.shape, spread.dtype),
        cost_estimate=pl.CostEstimate(flops=1_000_000, bytes_accessed=2_000_000, transcendentals=0),
        compiler_params=pltpu.CompilerParams(vmem_limit_bytes=12 * 1024 * 1024),
        name="pick",
    )(section_to_group, spread)


def multiply_kernel(me_ref, inputs_ref, routed_ref, out_ref, rows_ref):
    me = me_ref[0]
    shards, piece, width = routed_ref.shape
    heads, depth = KVH, width // KVH
    per_head = shards // heads
    own = inputs_ref.shape[1]
    block_rows = ROWS // per_head
    for d in range(shards):
        rows_ref[d * own : (d + 1) * own, :] = inputs_ref[me ^ d].astype(jnp.float32)
    inputs = rows_ref[...].astype(jnp.bfloat16)
    for h in range(heads):
        tiles = [
            routed_ref[:, :, (i * heads + h) * ROW_TILE : (i * heads + h + 1) * ROW_TILE]
            for i in range(depth // ROW_TILE)
        ]
        product = lax.dot_general(
            inputs,
            jnp.concatenate(tiles, axis=-1).reshape(shards * piece, depth),
            (((1,), (1,)), ((), ())),
            preferred_element_type=jnp.float32,
        )
        for i in range(per_head):
            r = me ^ (h * per_head + i)
            out_ref[r & 1, r >> 2, (r >> 1) & 1] = product[i * block_rows : (i + 1) * block_rows]


def multiply(me, inputs, routed):
    shards, _, width = routed.shape
    heads, depth = KVH, width // KVH
    return pl.pallas_call(
        multiply_kernel,
        in_specs=[pl.BlockSpec(memory_space=pltpu.SMEM), VMEM, VMEM],
        out_specs=VMEM,
        out_shape=jax.ShapeDtypeStruct((2, 8, 2, ROWS * heads // shards, 2 * HD), jnp.float32),
        scratch_shapes=[pltpu.VMEM((ROWS, depth), jnp.float32)],
        compiler_params=pltpu.CompilerParams(vmem_limit_bytes=12 * 1024 * 1024),
        cost_estimate=pl.CostEstimate(
            flops=2 * ROWS * heads * 2 * HD * depth, bytes_accessed=3_000_000, transcendentals=0
        ),
        name="multiply",
    )(me, inputs, routed)


def reduce_rows(partial):
    shards = lax.axis_size("shard")

    def send(values, bits):
        return lax.ppermute(values, "shard", [(i, i ^ bits) for i in range(shards)])

    partial = partial[0] + send(partial[1], 1)
    head = lax.reduce_precision(partial[1:], 8, 7)
    rest = partial[1:, :, :, :HD] - head[:, :, :, :HD]
    halves = jnp.concatenate([head, rest], axis=-1).astype(jnp.bfloat16)
    arrived = {}
    for k in (4, 5, 3, 6, 2, 7, 1):
        if k == 4:
            arrived[k] = send(halves[k - 1, ::-1], 9 << 1)
        else:
            arrived[k] = send(halves[k - 1], k << 2)
    total = sum(v.astype(jnp.float32) for v in arrived.values())
    keys = total[:, :, :HD] + total[:, :, 2 * HD :]
    partial = partial[0] + jnp.concatenate([keys, total[:, :, HD : 2 * HD]], axis=-1)
    partial = partial[0] + send(partial[1], 1 << 1)
    return partial


def step(train_weights, section_to_group, hidden, queries, kv_cache, lengths):
    shards = lax.axis_size("shard")
    sections = lax.axis_size("section")
    per_head = shards // KVH
    row_block = ROWS // per_head
    piece_cols = 2 * HD // shards
    slice_rows = train_weights.shape[1]
    me = lax.axis_index("shard").astype(jnp.int32).reshape(1)
    flipped, keep, other = enter(me, train_weights, hidden, shards)
    inputs = spread_rows(keep, other)
    flipped = flipped.reshape(sections, -1, KVH * slice_rows)
    spread = exchange(flipped, "section")
    picked = pick(section_to_group, spread)
    routed = exchange(picked, "section").reshape(shards, piece_cols, KVH * slice_rows)
    received = exchange(routed, "shard")
    layer_out = received.reshape(shards, piece_cols, -1, KVH, ROW_TILE)
    layer_out = layer_out.transpose(3, 1, 0, 2, 4).reshape(1, KVH, piece_cols, D)
    fresh = reduce_rows(multiply(me, inputs, routed)).astype(jnp.bfloat16)
    block_index = lax.axis_index("shard") % per_head
    row_lengths = lax.dynamic_slice_in_dim(lengths, block_index * row_block, row_block, 0)
    query_rows = queries.reshape(row_block, QPK, HD)
    context = attend(query_rows, kv_cache, fresh, row_lengths)
    return (context, layer_out)


def solution(mesh):
    return jax.shard_map(
        step,
        mesh=mesh,
        in_specs=(
            P("section", "shard", None),
            P(),
            P(("section", "shard"), None),
            P(("section", "shard"), None),
            P(("section", "shard"), None, None),
            P("section"),
        ),
        out_specs=(P(("section", "shard"), None), P("section", None, "shard", None)),
        check_vma=False,
    )
```

profile of v0, /device:TPU:32, one launch (start us, length us, event | category | flops | bytes accessed | tf_op | source)
XLA Modules:
  0.0 174.5 jit_solution(13216471984741088247)
XLA Ops:
  0.6 3.3 %enter.1 = (bf16[32,8,2048]{2,1,0:T(8,128)(2,1)}, bf16[4,4,4,512]{3,2,1,0:T(4,128)(2,1)}, bf16[4,4,4,512]{3,2,1,0:T(4,128)(2,1)}) custom-call(s32[1]{0:T(128)} %bitcast.me_ref, f32[1,512,1024]{2,1,0:T(8,128)} %weights_ref.1, bf16[4,16384]{1,0:T(4,128)(2,1)} %hidden_ref.1), custom_call_target="tpu_custom_call" | custom-call | flops 2000000 | bytes 3000000 | tf_op jit(solution)/shard_map/enter/pallas_call | solution.py:118
  4.0 0.0 copy-start.2
  4.0 5.1 %collective-permute-start = (bf16[4,4,4,512]{3,2,1,0:T(4,128)(2,1)}, bf16[4,4,4,512]{3,2,1,0:T(4,128)(2,1)S(1)}, u32[]{:S(2)}, u32[]{:S(2)}) collective-permute-start(bf16[4,4,4,512]{3,2,1,0:T(4,128)(2,1)} %get-tuple-element.6), channel_id=1, source_target_pairs={{0,1},{1,0},{2,3},{3,2},{4,5},{5,4},{6,7},{7,6},{8,9},{9,8},{10,11... | collective-permute-start | bytes 196616 | tf_op jit(solution)/shard_map/ppermute | solution.py:28
  9.1 4.6 %all-to-all-start = ((bf16[16,16,2048]{2,1,0:T(8,128)(2,1)}), bf16[16,16,2048]{2,1,0:T(8,128)(2,1)S(1)}, u32[]{:S(2)}, u32[]{:S(2)}) async-start(bf16[16,16,2048]{2,1,0:T(8,128)(2,1)} %bitcast.104), calls=%async_computation | async-start | bytes 2097152 | tf_op jit(solution)/shard_map/all_to_all | solution.py:21
  13.9 5.2 %collective-permute-start.2 = (bf16[2,4,4,512]{3,2,0,1:T(4,128)(2,1)S(1)}, bf16[2,4,4,512]{3,2,0,1:T(4,128)(2,1)S(1)}, u32[]{:S(2)}, u32[]{:S(2)}) collective-permute-start(bf16[2,4,4,512]{3,2,0,1:T(4,128)(2,1)S(1)} %pad_maximum_fusion.1), channel_id=1, source_target_pairs={{0,4},{1,5},{2,6},{3,7},{4,0},{5,1},{6,2},{7,3},{8,12},{9,13},{10,... | collective-permute-start | bytes 98312 | tf_op jit(solution)/shard_map/ppermute | solution.py:28
  19.1 2.3 %collective-permute-start.1 = (bf16[2,4,4,512]{3,2,0,1:T(4,128)(2,1)S(1)}, bf16[2,4,4,512]{3,2,0,1:T(4,128)(2,1)S(1)}, u32[]{:S(2)}, u32[]{:S(2)}) collective-permute-start(bf16[2,4,4,512]{3,2,0,1:T(4,128)(2,1)S(1)} %pad_maximum_fusion), channel_id=1, source_target_pairs={{0,2},{1,3},{2,0},{3,1},{4,6},{5,7},{6,4},{7,5},{8,10},{9,11},{10,... | collective-permute-start | bytes 98312 | tf_op jit(solution)/shard_map/ppermute | solution.py:28
  21.5 3.4 %collective-permute-start.3 = (bf16[2,4,4,512]{3,2,1,0:T(4,128)(2,1)S(1)}, bf16[2,4,4,512]{3,2,1,0:T(4,128)(2,1)S(1)}, u32[]{:S(2)}, u32[]{:S(2)}) collective-permute-start(bf16[2,4,4,512]{3,2,1,0:T(4,128)(2,1)S(1)} %pad_maximum_fusion.2), channel_id=1, source_target_pairs={{0,6},{1,7},{2,4},{3,5},{4,2},{5,3},{6,0},{7,1},{8,14},{9,15},{10,... | collective-permute-start | bytes 98312 | tf_op jit(solution)/shard_map/ppermute | solution.py:28
  24.9 0.0 collective-permute-done.2
  24.9 0.0 collective-permute-done.1
  24.9 2.4 %collective-permute-done.3 = bf16[2,4,4,512]{3,2,1,0:T(4,128)(2,1)S(1)} collective-permute-done((bf16[2,4,4,512]{3,2,1,0:T(4,128)(2,1)S(1)}, bf16[2,4,4,512]{3,2,1,0:T(4,128)(2,1)S(1)}, u32[]{:S(2)}, u32[]{:S(2)}) %collective-permute-start.3) | collective-permute-done | bytes 32800 | tf_op jit(solution)/shard_map/ppermute | solution.py:28
  27.3 8.8 %collective-permute-start.4 = (bf16[4,2,4,512]{3,2,1,0:T(4,128)(2,1)S(1)}, bf16[4,2,4,512]{3,2,1,0:T(4,128)(2,1)S(1)}, u32[]{:S(2)}, u32[]{:S(2)}) collective-permute-start(bf16[4,2,4,512]{3,2,1,0:T(4,128)(2,1)S(1)} %pad_maximum_fusion.3), channel_id=1, source_target_pairs={{0,8},{1,9},{2,10},{3,11},{4,12},{5,13},{6,14},{7,15},{8,0},{9,1},... | collective-permute-start | bytes 98312 | tf_op jit(solution)/shard_map/ppermute | solution.py:28
  36.2 9.5 %collective-permute-start.5 = (bf16[4,2,4,512]{3,2,1,0:T(4,128)(2,1)S(1)}, bf16[4,2,4,512]{3,2,1,0:T(4,128)(2,1)S(1)}, u32[]{:S(2)}, u32[]{:S(2)}) collective-permute-start(bf16[4,2,4,512]{3,2,1,0:T(4,128)(2,1)S(1)} %pad_maximum_fusion.4), channel_id=1, source_target_pairs={{0,16},{1,17},{2,18},{3,19},{4,20},{5,21},{6,22},{7,23},{8,24},{9,... | collective-permute-start | bytes 98312 | tf_op jit(solution)/shard_map/ppermute | solution.py:28
  45.7 1.9 %collective-permute-start.6 = (bf16[4,2,4,512]{3,2,1,0:T(4,128)(2,1)S(1)}, bf16[4,2,4,512]{3,2,1,0:T(4,128)(2,1)S(1)}, u32[]{:S(2)}, u32[]{:S(2)}) collective-permute-start(bf16[4,2,4,512]{3,2,1,0:T(4,128)(2,1)S(1)} %pad_maximum_fusion.5), channel_id=1, source_target_pairs={{0,24},{1,25},{2,26},{3,27},{4,28},{5,29},{6,30},{7,31},{8,16},{9,... | collective-permute-start | bytes 98312 | tf_op jit(solution)/shard_map/ppermute | solution.py:28
  47.6 0.0 all-to-all-done.spread_ref
  47.6 1.7 pick.1
  49.3 5.7 %all-to-all-start.1 = ((bf16[16,16,2048]{2,1,0:T(8,128)(2,1)}), bf16[16,16,2048]{2,1,0:T(8,128)(2,1)}, u32[]{:S(2)}, u32[]{:S(2)}) async-start(bf16[16,16,2048]{2,1,0:T(8,128)(2,1)} %pick.1), calls=%async_computation.1 | async-start | bytes 2097152 | tf_op jit(solution)/shard_map/all_to_all | solution.py:21
  55.0 0.0 collective-permute-done.4
  55.1 0.0 collective-permute-done.5
  55.1 0.3 collective-permute-done.6
  55.4 16.2 %all-to-all-done.1 = bf16[16,16,2048]{2,1,0:T(8,128)(2,1)} async-done(((bf16[16,16,2048]{2,1,0:T(8,128)(2,1)}), bf16[16,16,2048]{2,1,0:T(8,128)(2,1)}, u32[]{:S(2)}, u32[]{:S(2)}) %all-to-all-start.1) | async-done | bytes 1048608 | tf_op jit(solution)/shard_map/all_to_all | solution.py:21
  71.6 1.7 multiply.1
  73.3 0.0 copy-start.4
  73.3 0.0 copy-start.3
  73.4 0.0 copy-start.1
  73.4 4.0 %collective-permute-start.7 = (f32[8,2,16,256]{3,2,1,0:T(8,128)S(1)}, f32[8,2,16,256]{3,2,1,0:T(8,128)S(1)}, u32[]{:S(2)}, u32[]{:S(2)}) collective-permute-start(f32[8,2,16,256]{3,2,1,0:T(8,128)S(1)} %slice_bitcast_fusion), channel_id=1, source_target_pairs={{0,1},{1,0},{2,3},{3,2},{4,5},{5,4},{6,7},{7,6},{8,9},{9,8},{10,11... | collective-permute-start | bytes 786440 | tf_op jit(solution)/shard_map/ppermute | solution.py:206
  77.4 13.8 %all-to-all-start.2 = ((bf16[32,8,2048]{2,1,0:T(8,128)(2,1)}), bf16[32,8,2048]{2,1,0:T(8,128)(2,1)S(1)}, u32[]{:S(2)}, u32[]{:S(2)}) async-start(bf16[32,8,2048]{2,1,0:T(8,128)(2,1)} %bitcast.19.routed_ref), calls=%async_computation.2 | async-start | bytes 2097152 | tf_op jit(solution)/shard_map/all_to_all | solution.py:21
  91.3 0.0 collective-permute-done.7
  91.4 11.2 %collective-permute-start.8 = (bf16[2,16,384]{2,1,0:T(8,128)(2,1)S(1)}, bf16[2,16,384]{2,1,0:T(8,128)(2,1)S(1)}, u32[]{:S(2)}, u32[]{:S(2)}) collective-permute-start(bf16[2,16,384]{2,1,0:T(8,128)(2,1)S(1)} %reverse_bitcast_fusion), channel_id=1, source_target_pairs={{0,18},{1,19},{2,16},{3,17},{4,22},{5,23},{6,20},{7,21},{8,26},{9,... | collective-permute-start | bytes 73736 | tf_op jit(solution)/shard_map/ppermute | solution.py:206
  102.6 2.5 %collective-permute-start.10 = (bf16[2,16,384]{2,1,0:T(8,128)(2,1)S(1)}, bf16[2,16,384]{2,1,0:T(8,128)(2,1)S(1)}, u32[]{:S(2)}, u32[]{:S(2)}) collective-permute-start(bf16[2,16,384]{2,1,0:T(8,128)(2,1)S(1)} %get-tuple-element.12), channel_id=1, source_target_pairs={{0,12},{1,13},{2,14},{3,15},{4,8},{5,9},{6,10},{7,11},{8,4},{9,5},... | collective-permute-start | bytes 73736 | tf_op jit(solution)/shard_map/ppermute | solution.py:206
  105.2 0.1 dynamic_slice.3
  105.3 2.4 %collective-permute-start.11 = (bf16[2,16,384]{2,1,0:T(8,128)(2,1)S(1)}, bf16[2,16,384]{2,1,0:T(8,128)(2,1)S(1)}, u32[]{:S(2)}, u32[]{:S(2)}) collective-permute-start(bf16[2,16,384]{2,1,0:T(8,128)(2,1)S(1)} %get-tuple-element.13), channel_id=1, source_target_pairs={{0,24},{1,25},{2,26},{3,27},{4,28},{5,29},{6,30},{7,31},{8,16},{9,... | collective-permute-start | bytes 73736 | tf_op jit(solution)/shard_map/ppermute | solution.py:206
  107.7 9.1 %collective-permute-start.12 = (bf16[2,16,384]{2,1,0:T(8,128)(2,1)S(1)}, bf16[2,16,384]{2,1,0:T(8,128)(2,1)S(1)}, u32[]{:S(2)}, u32[]{:S(2)}) collective-permute-start(bf16[2,16,384]{2,1,0:T(8,128)(2,1)S(1)} %get-tuple-element.14), channel_id=1, source_target_pairs={{0,8},{1,9},{2,10},{3,11},{4,12},{5,13},{6,14},{7,15},{8,0},{9,1},... | collective-permute-start | bytes 73736 | tf_op jit(solution)/shard_map/ppermute | solution.py:206
  116.8 5.5 %collective-permute-start.13 = (bf16[2,16,384]{2,1,0:T(8,128)(2,1)S(1)}, bf16[2,16,384]{2,1,0:T(8,128)(2,1)S(1)}, u32[]{:S(2)}, u32[]{:S(2)}) collective-permute-start(bf16[2,16,384]{2,1,0:T(8,128)(2,1)S(1)} %get-tuple-element.16), channel_id=1, source_target_pairs={{0,28},{1,29},{2,30},{3,31},{4,24},{5,25},{6,26},{7,27},{8,20},{9,... | collective-permute-start | bytes 73736 | tf_op jit(solution)/shard_map/ppermute | solution.py:206
  122.3 27.5 %collective-permute-done.8 = bf16[2,16,384]{2,1,0:T(8,128)(2,1)S(1)} collective-permute-done((bf16[2,16,384]{2,1,0:T(8,128)(2,1)S(1)}, bf16[2,16,384]{2,1,0:T(8,128)(2,1)S(1)}, u32[]{:S(2)}, u32[]{:S(2)}) %collective-permute-start.8) | collective-permute-done | bytes 24608 | tf_op jit(solution)/shard_map/ppermute | solution.py:206
  149.7 3.9 %collective-permute-start.14 = (bf16[2,16,384]{2,1,0:T(8,128)(2,1)S(1)}, bf16[2,16,384]{2,1,0:T(8,128)(2,1)S(1)}, u32[]{:S(2)}, u32[]{:S(2)}) collective-permute-start(bf16[2,16,384]{2,1,0:T(8,128)(2,1)S(1)} %get-tuple-element.15), channel_id=1, source_target_pairs={{0,4},{1,5},{2,6},{3,7},{4,0},{5,1},{6,2},{7,3},{8,12},{9,13},{10,... | collective-permute-start | bytes 73736 | tf_op jit(solution)/shard_map/ppermute | solution.py:206
  153.6 0.0 collective-permute-done.10
  153.6 1.9 %collective-permute-start.9 = (bf16[2,16,384]{2,1,0:T(8,128)(2,1)S(1)}, bf16[2,16,384]{2,1,0:T(8,128)(2,1)S(1)}, u32[]{:S(2)}, u32[]{:S(2)}) collective-permute-start(bf16[2,16,384]{2,1,0:T(8,128)(2,1)S(1)} %get-tuple-element.11), channel_id=1, source_target_pairs={{0,20},{1,21},{2,22},{3,23},{4,16},{5,17},{6,18},{7,19},{8,28},{9,... | collective-permute-start | bytes 73736 | tf_op jit(solution)/shard_map/ppermute | solution.py:206
  155.6 0.1 iota_compare_fusion
  155.7 0.6 collective-permute-done.14
  156.3 10.0 %collective-permute-done.9 = bf16[2,16,384]{2,1,0:T(8,128)(2,1)S(1)} collective-permute-done((bf16[2,16,384]{2,1,0:T(8,128)(2,1)S(1)}, bf16[2,16,384]{2,1,0:T(8,128)(2,1)S(1)}, u32[]{:S(2)}, u32[]{:S(2)}) %collective-permute-start.9) | collective-permute-done | bytes 24608 | tf_op jit(solution)/shard_map/ppermute | solution.py:206
  166.4 1.9 %collective-permute-start.15 = (f32[16,256]{1,0:T(8,128)S(1)}, f32[16,256]{1,0:T(8,128)S(1)}, u32[]{:S(2)}, u32[]{:S(2)}) collective-permute-start(f32[16,256]{1,0:T(8,128)S(1)} %slice_bitcast_fusion.3), channel_id=1, source_target_pairs={{0,2},{1,3},{2,0},{3,1},{4,6},{5,7},{6,4},{7,5},{8,10},{9,11},{10,... | collective-permute-start | bytes 49160 | tf_op jit(solution)/shard_map/ppermute | solution.py:206
  168.3 0.5 fusion.40
  168.8 3.2 %collective-permute-done.15 = f32[16,256]{1,0:T(8,128)S(1)} collective-permute-done((f32[16,256]{1,0:T(8,128)S(1)}, f32[16,256]{1,0:T(8,128)S(1)}, u32[]{:S(2)}, u32[]{:S(2)}) %collective-permute-start.15) | collective-permute-done | bytes 16416 | tf_op jit(solution)/shard_map/ppermute | solution.py:206
  172.0 0.1 fusion.30
  172.2 0.2 fusion.6
  172.4 0.3 fusion.1
  172.7 0.7 copy.33
  173.4 1.2 copy.17
  (46 shorter events, 0.6 us)
Async XLA Ops:
  0.6 47.0 %copy-start = (s32[16]{0:T(128)S(1)}, s32[16]{0:T(128)}, u32[]{:S(2)}) copy-start(s32[16]{0:T(128)} %group_ref.1) | copy-start | bytes 196
  4.0 9.7 %copy-start.2 = (bf16[4,4,4,512]{3,2,1,0:T(4,128)(2,1)S(1)}, bf16[4,4,4,512]{3,2,1,0:T(4,128)(2,1)}, u32[]{:S(2)}) copy-start(bf16[4,4,4,512]{3,2,1,0:T(4,128)(2,1)} %get-tuple-element.5) | copy-start | bytes 196612
  4.0 9.8 %collective-permute-start = (bf16[4,4,4,512]{3,2,1,0:T(4,128)(2,1)}, bf16[4,4,4,512]{3,2,1,0:T(4,128)(2,1)S(1)}, u32[]{:S(2)}, u32[]{:S(2)}) collective-permute-start(bf16[4,4,4,512]{3,2,1,0:T(4,128)(2,1)} %get-tuple-element.6), channel_id=1, source_target_pairs={{0,1},{1,0},{2,3},{3,2},{4,5},{5,4},{6,7},{7,6},{8,9},{9,8},{10,11... | collective-permute-start | bytes 196616 | tf_op jit(solution)/shard_map/ppermute | solution.py:28
  9.1 38.5 %all-to-all-start = ((bf16[16,16,2048]{2,1,0:T(8,128)(2,1)}), bf16[16,16,2048]{2,1,0:T(8,128)(2,1)S(1)}, u32[]{:S(2)}, u32[]{:S(2)}) async-start(bf16[16,16,2048]{2,1,0:T(8,128)(2,1)} %bitcast.104), calls=%async_computation | async-start | bytes 2097152 | tf_op jit(solution)/shard_map/all_to_all | solution.py:21
  13.9 11.0 %collective-permute-start.2 = (bf16[2,4,4,512]{3,2,0,1:T(4,128)(2,1)S(1)}, bf16[2,4,4,512]{3,2,0,1:T(4,128)(2,1)S(1)}, u32[]{:S(2)}, u32[]{:S(2)}) collective-permute-start(bf16[2,4,4,512]{3,2,0,1:T(4,128)(2,1)S(1)} %pad_maximum_fusion.1), channel_id=1, source_target_pairs={{0,4},{1,5},{2,6},{3,7},{4,0},{5,1},{6,2},{7,3},{8,12},{9,13},{10,... | collective-permute-start | bytes 98312 | tf_op jit(solution)/shard_map/ppermute | solution.py:28
  19.1 5.8 %collective-permute-start.1 = (bf16[2,4,4,512]{3,2,0,1:T(4,128)(2,1)S(1)}, bf16[2,4,4,512]{3,2,0,1:T(4,128)(2,1)S(1)}, u32[]{:S(2)}, u32[]{:S(2)}) collective-permute-start(bf16[2,4,4,512]{3,2,0,1:T(4,128)(2,1)S(1)} %pad_maximum_fusion), channel_id=1, source_target_pairs={{0,2},{1,3},{2,0},{3,1},{4,6},{5,7},{6,4},{7,5},{8,10},{9,11},{10,... | collective-permute-start | bytes 98312 | tf_op jit(solution)/shard_map/ppermute | solution.py:28
  21.5 5.8 %collective-permute-start.3 = (bf16[2,4,4,512]{3,2,1,0:T(4,128)(2,1)S(1)}, bf16[2,4,4,512]{3,2,1,0:T(4,128)(2,1)S(1)}, u32[]{:S(2)}, u32[]{:S(2)}) collective-permute-start(bf16[2,4,4,512]{3,2,1,0:T(4,128)(2,1)S(1)} %pad_maximum_fusion.2), channel_id=1, source_target_pairs={{0,6},{1,7},{2,4},{3,5},{4,2},{5,3},{6,0},{7,1},{8,14},{9,15},{10,... | collective-permute-start | bytes 98312 | tf_op jit(solution)/shard_map/ppermute | solution.py:28
  27.3 27.7 %collective-permute-start.4 = (bf16[4,2,4,512]{3,2,1,0:T(4,128)(2,1)S(1)}, bf16[4,2,4,512]{3,2,1,0:T(4,128)(2,1)S(1)}, u32[]{:S(2)}, u32[]{:S(2)}) collective-permute-start(bf16[4,2,4,512]{3,2,1,0:T(4,128)(2,1)S(1)} %pad_maximum_fusion.3), channel_id=1, source_target_pairs={{0,8},{1,9},{2,10},{3,11},{4,12},{5,13},{6,14},{7,15},{8,0},{9,1},... | collective-permute-start | bytes 98312 | tf_op jit(solution)/shard_map/ppermute | solution.py:28
  36.2 18.9 %collective-permute-start.5 = (bf16[4,2,4,512]{3,2,1,0:T(4,128)(2,1)S(1)}, bf16[4,2,4,512]{3,2,1,0:T(4,128)(2,1)S(1)}, u32[]{:S(2)}, u32[]{:S(2)}) collective-permute-start(bf16[4,2,4,512]{3,2,1,0:T(4,128)(2,1)S(1)} %pad_maximum_fusion.4), channel_id=1, source_target_pairs={{0,16},{1,17},{2,18},{3,19},{4,20},{5,21},{6,22},{7,23},{8,24},{9,... | collective-permute-start | bytes 98312 | tf_op jit(solution)/shard_map/ppermute | solution.py:28
  45.7 9.7 %collective-permute-start.6 = (bf16[4,2,4,512]{3,2,1,0:T(4,128)(2,1)S(1)}, bf16[4,2,4,512]{3,2,1,0:T(4,128)(2,1)S(1)}, u32[]{:S(2)}, u32[]{:S(2)}) collective-permute-start(bf16[4,2,4,512]{3,2,1,0:T(4,128)(2,1)S(1)} %pad_maximum_fusion.5), channel_id=1, source_target_pairs={{0,24},{1,25},{2,26},{3,27},{4,28},{5,29},{6,30},{7,31},{8,16},{9,... | collective-permute-start | bytes 98312 | tf_op jit(solution)/shard_map/ppermute | solution.py:28
  49.3 22.3 %all-to-all-start.1 = ((bf16[16,16,2048]{2,1,0:T(8,128)(2,1)}), bf16[16,16,2048]{2,1,0:T(8,128)(2,1)}, u32[]{:S(2)}, u32[]{:S(2)}) async-start(bf16[16,16,2048]{2,1,0:T(8,128)(2,1)} %pick.1), calls=%async_computation.1 | async-start | bytes 2097152 | tf_op jit(solution)/shard_map/all_to_all | solution.py:21
  73.3 31.9 %copy-start.4 = (s32[128]{0:T(128)S(1)}, s32[128]{0:T(128)}, u32[]{:S(2)}) copy-start(s32[128]{0:T(128)} %param.11) | copy-start | bytes 1540
  73.3 82.3 %copy-start.3 = (bf16[16,2048]{1,0:T(8,128)(2,1)S(1)}, bf16[16,2048]{1,0:T(8,128)(2,1)}, u32[]{:S(2)}) copy-start(bf16[16,2048]{1,0:T(8,128)(2,1)} %param.9) | copy-start | bytes 196612
  73.4 94.9 %copy-start.1 = (bf16[16,128,256]{2,1,0:T(8,128)(2,1)S(1)}, bf16[16,128,256]{2,1,0:T(8,128)(2,1)}, u32[]{:S(2)}) copy-start(bf16[16,128,256]{2,1,0:T(8,128)(2,1)} %param.10) | copy-start | bytes 3145732
  73.4 17.9 %collective-permute-start.7 = (f32[8,2,16,256]{3,2,1,0:T(8,128)S(1)}, f32[8,2,16,256]{3,2,1,0:T(8,128)S(1)}, u32[]{:S(2)}, u32[]{:S(2)}) collective-permute-start(f32[8,2,16,256]{3,2,1,0:T(8,128)S(1)} %slice_bitcast_fusion), channel_id=1, source_target_pairs={{0,1},{1,0},{2,3},{3,2},{4,5},{5,4},{6,7},{7,6},{8,9},{9,8},{10,11... | collective-permute-start | bytes 786440 | tf_op jit(solution)/shard_map/ppermute | solution.py:206
  77.4 95.9 %all-to-all-start.2 = ((bf16[32,8,2048]{2,1,0:T(8,128)(2,1)}), bf16[32,8,2048]{2,1,0:T(8,128)(2,1)S(1)}, u32[]{:S(2)}, u32[]{:S(2)}) async-start(bf16[32,8,2048]{2,1,0:T(8,128)(2,1)} %bitcast.19.routed_ref), calls=%async_computation.2 | async-start | bytes 2097152 | tf_op jit(solution)/shard_map/all_to_all | solution.py:21
  91.4 58.3 %collective-permute-start.8 = (bf16[2,16,384]{2,1,0:T(8,128)(2,1)S(1)}, bf16[2,16,384]{2,1,0:T(8,128)(2,1)S(1)}, u32[]{:S(2)}, u32[]{:S(2)}) collective-permute-start(bf16[2,16,384]{2,1,0:T(8,128)(2,1)S(1)} %reverse_bitcast_fusion), channel_id=1, source_target_pairs={{0,18},{1,19},{2,16},{3,17},{4,22},{5,23},{6,20},{7,21},{8,26},{9,... | collective-permute-start | bytes 73736 | tf_op jit(solution)/shard_map/ppermute | solution.py:206
  102.6 51.0 %collective-permute-start.10 = (bf16[2,16,384]{2,1,0:T(8,128)(2,1)S(1)}, bf16[2,16,384]{2,1,0:T(8,128)(2,1)S(1)}, u32[]{:S(2)}, u32[]{:S(2)}) collective-permute-start(bf16[2,16,384]{2,1,0:T(8,128)(2,1)S(1)} %get-tuple-element.12), channel_id=1, source_target_pairs={{0,12},{1,13},{2,14},{3,15},{4,8},{5,9},{6,10},{7,11},{8,4},{9,5},... | collective-permute-start | bytes 73736 | tf_op jit(solution)/shard_map/ppermute | solution.py:206
  105.3 50.4 %collective-permute-start.11 = (bf16[2,16,384]{2,1,0:T(8,128)(2,1)S(1)}, bf16[2,16,384]{2,1,0:T(8,128)(2,1)S(1)}, u32[]{:S(2)}, u32[]{:S(2)}) collective-permute-start(bf16[2,16,384]{2,1,0:T(8,128)(2,1)S(1)} %get-tuple-element.13), channel_id=1, source_target_pairs={{0,24},{1,25},{2,26},{3,27},{4,28},{5,29},{6,30},{7,31},{8,16},{9,... | collective-permute-start | bytes 73736 | tf_op jit(solution)/shard_map/ppermute | solution.py:206
  107.7 48.0 %collective-permute-start.12 = (bf16[2,16,384]{2,1,0:T(8,128)(2,1)S(1)}, bf16[2,16,384]{2,1,0:T(8,128)(2,1)S(1)}, u32[]{:S(2)}, u32[]{:S(2)}) collective-permute-start(bf16[2,16,384]{2,1,0:T(8,128)(2,1)S(1)} %get-tuple-element.14), channel_id=1, source_target_pairs={{0,8},{1,9},{2,10},{3,11},{4,12},{5,13},{6,14},{7,15},{8,0},{9,1},... | collective-permute-start | bytes 73736 | tf_op jit(solution)/shard_map/ppermute | solution.py:206
  116.8 38.9 %collective-permute-start.13 = (bf16[2,16,384]{2,1,0:T(8,128)(2,1)S(1)}, bf16[2,16,384]{2,1,0:T(8,128)(2,1)S(1)}, u32[]{:S(2)}, u32[]{:S(2)}) collective-permute-start(bf16[2,16,384]{2,1,0:T(8,128)(2,1)S(1)} %get-tuple-element.16), channel_id=1, source_target_pairs={{0,28},{1,29},{2,30},{3,31},{4,24},{5,25},{6,26},{7,27},{8,20},{9,... | collective-permute-start | bytes 73736 | tf_op jit(solution)/shard_map/ppermute | solution.py:206
  149.7 6.6 %collective-permute-start.14 = (bf16[2,16,384]{2,1,0:T(8,128)(2,1)S(1)}, bf16[2,16,384]{2,1,0:T(8,128)(2,1)S(1)}, u32[]{:S(2)}, u32[]{:S(2)}) collective-permute-start(bf16[2,16,384]{2,1,0:T(8,128)(2,1)S(1)} %get-tuple-element.15), channel_id=1, source_target_pairs={{0,4},{1,5},{2,6},{3,7},{4,0},{5,1},{6,2},{7,3},{8,12},{9,13},{10,... | collective-permute-start | bytes 73736 | tf_op jit(solution)/shard_map/ppermute | solution.py:206
  153.6 12.7 %collective-permute-start.9 = (bf16[2,16,384]{2,1,0:T(8,128)(2,1)S(1)}, bf16[2,16,384]{2,1,0:T(8,128)(2,1)S(1)}, u32[]{:S(2)}, u32[]{:S(2)}) collective-permute-start(bf16[2,16,384]{2,1,0:T(8,128)(2,1)S(1)} %get-tuple-element.11), channel_id=1, source_target_pairs={{0,20},{1,21},{2,22},{3,23},{4,16},{5,17},{6,18},{7,19},{8,28},{9,... | collective-permute-start | bytes 73736 | tf_op jit(solution)/shard_map/ppermute | solution.py:206
  166.4 5.6 %collective-permute-start.15 = (f32[16,256]{1,0:T(8,128)S(1)}, f32[16,256]{1,0:T(8,128)S(1)}, u32[]{:S(2)}, u32[]{:S(2)}) collective-permute-start(f32[16,256]{1,0:T(8,128)S(1)} %slice_bitcast_fusion.3), channel_id=1, source_target_pairs={{0,2},{1,3},{2,0},{3,1},{4,6},{5,7},{6,4},{7,5},{8,10},{9,11},{10,... | collective-permute-start | bytes 49160 | tf_op jit(solution)/shard_map/ppermute | solution.py:206
where the time goes:
time: 175 us
  starting transfers between devices  103 us (59%)
  waiting for transfers between devices  60.2 us (34%)
  Pallas kernels  6.71 us (4%)
  local copies, waits for them, and re-layouts  2.16 us (1%)
    ppermute x16, starting transfers between devices, send(): return lax.ppermute(values, 'shard', [(i, i ^ bits) for i in range(shards)])  78.6 us
    ppermute x16, waiting for transfers between devices, send(): return lax.ppermute(values, 'shard', [(i, i ^ bits) for i in range(shards)])  44 us
    all_to_all x3, starting transfers between devices, exchange(): return lax.all_to_all(blocks, axis, split_axis=0, concat_axis=0, tiled=True)  24.2 us
    all_to_all x3, waiting for transfers between devices, exchange(): return lax.all_to_all(blocks, axis, split_axis=0, concat_axis=0, tiled=True)  16.2 us
  transfers between devices with their start and end apart: 19, of which 7 were waited for; matrix products, arithmetic and copies ran while one was open for 1% of the time, Pallas kernels for 1%

commit v1 on v0

--- a/solution.py
+++ b/solution.py
@@ -156,7 +156,7 @@
     )(section_to_group, spread)
 
 
-def multiply_kernel(me_ref, inputs_ref, routed_ref, out_ref, rows_ref):
+def multiply_kernel(me_ref, inputs_ref, routed_ref, even_ref, odd_ref, rows_ref):
     me = me_ref[0]
     shards, piece, width = routed_ref.shape
     heads, depth = KVH, width // KVH
@@ -179,7 +179,16 @@
         )
         for i in range(per_head):
             r = me ^ (h * per_head + i)
-            out_ref[r & 1, r >> 2, (r >> 1) & 1] = product[i * block_rows : (i + 1) * block_rows]
+            value = product[i * block_rows : (i + 1) * block_rows]
+            own_side = (r & 1) == 0
+
+            @pl.when(own_side)
+            def _():
+                even_ref[r >> 2, (r >> 1) & 1] = value
+
+            @pl.when(jnp.logical_not(own_side))
+            def _():
+                odd_ref[r >> 2, (r >> 1) & 1] = value
 
 
 def multiply(me, inputs, routed):
@@ -188,8 +197,8 @@
     return pl.pallas_call(
         multiply_kernel,
         in_specs=[pl.BlockSpec(memory_space=pltpu.SMEM), VMEM, VMEM],
-        out_specs=VMEM,
-        out_shape=jax.ShapeDtypeStruct((2, 8, 2, ROWS * heads // shards, 2 * HD), jnp.float32),
+        out_specs=[VMEM, VMEM],
+        out_shape=[jax.ShapeDtypeStruct((8, 2, ROWS * heads // shards, 2 * HD), jnp.float32)] * 2,
         scratch_shapes=[pltpu.VMEM((ROWS, depth), jnp.float32)],
         compiler_params=pltpu.CompilerParams(vmem_limit_bytes=12 * 1024 * 1024),
         cost_estimate=pl.CostEstimate(
@@ -199,22 +208,19 @@
     )(me, inputs, routed)
 
 
-def reduce_rows(partial):
+def reduce_rows(even, odd):
     shards = lax.axis_size("shard")
 
     def send(values, bits):
         return lax.ppermute(values, "shard", [(i, i ^ bits) for i in range(shards)])
 
-    partial = partial[0] + send(partial[1], 1)
+    partial = even + send(odd, 1)
     head = lax.reduce_precision(partial[1:], 8, 7)
     rest = partial[1:, :, :, :HD] - head[:, :, :, :HD]
     halves = jnp.concatenate([head, rest], axis=-1).astype(jnp.bfloat16)
     arrived = {}
     for k in (4, 5, 3, 6, 2, 7, 1):
-        if k == 4:
-            arrived[k] = send(halves[k - 1, ::-1], 9 << 1)
-        else:
-            arrived[k] = send(halves[k - 1], k << 2)
+        arrived[k] = send(halves[k - 1], k << 2)
     total = sum(v.astype(jnp.float32) for v in arrived.values())
     keys = total[:, :, :HD] + total[:, :, 2 * HD :]
     partial = partial[0] + jnp.concatenate([keys, total[:, :, HD : 2 * HD]], axis=-1)
@@ -239,7 +245,7 @@
     received = exchange(routed, "shard")
     layer_out = received.reshape(shards, piece_cols, -1, KVH, ROW_TILE)
     layer_out = layer_out.transpose(3, 1, 0, 2, 4).reshape(1, KVH, piece_cols, D)
-    fresh = reduce_rows(multiply(me, inputs, routed)).astype(jnp.bfloat16)
+    fresh = reduce_rows(*multiply(me, inputs, routed)).astype(jnp.bfloat16)
     block_index = lax.axis_index("shard") % per_head
     row_lengths = lax.dynamic_slice_in_dim(lengths, block_index * row_block, row_block, 0)
     query_rows = queries.reshape(row_block, QPK, HD)

time: 175 us -> 154 us (0.88)
  the two profiles are of different devices: /device:TPU:32 before, /device:TPU:8 now
where the time goes in v1:
time: 154 us; the launch traced here: 153 us
  starting transfers between devices  102 us (66%)
  waiting for transfers between devices  38.4 us (25%)
  Pallas kernels  7.82 us (5%)
  local copies, waits for them, and re-layouts  2.14 us (1%)
    ppermute x16, starting transfers between devices, send(): return lax.ppermute(values, 'shard', [(i, i ^ bits) for i in range(shards)])  77.5 us
    ppermute x16, waiting for transfers between devices, send(): return lax.ppermute(values, 'shard', [(i, i ^ bits) for i in range(shards)])  38.4 us
    all_to_all x3, starting transfers between devices, exchange(): return lax.all_to_all(blocks, axis, split_axis=0, concat_axis=0, tiled=True)  24 us
    pallas_call x1, Pallas kernels, enter(): pl.pallas_call(enter_kernel, in_specs=[pl.BlockSpec(memory_space=pltpu.SM...  3.33 us
  transfers between devices with their start and end apart: 19, of which 6 were waited for; matrix products, arithmetic and copies ran while one was open for 2% of the time, Pallas kernels for 2%

profile of v1, /device:TPU:8, one launch (start us, length us, event | category | flops | bytes accessed | tf_op | source)
XLA Modules:
  0.0 152.7 jit_solution(3370136420404798835)
XLA Ops:
  0.6 3.3 %enter.1 = (bf16[32,8,2048]{2,1,0:T(8,128)(2,1)}, bf16[4,4,4,512]{3,2,1,0:T(4,128)(2,1)}, bf16[4,4,4,512]{3,2,1,0:T(4,128)(2,1)}) custom-call(s32[1]{0:T(128)} %bitcast.me_ref, f32[1,512,1024]{2,1,0:T(8,128)} %weights_ref.1, bf16[4,16384]{1,0:T(4,128)(2,1)} %hidden_ref.1), custom_call_target="tpu_custom_call" | custom-call | flops 2000000 | bytes 3000000 | tf_op jit(solution)/shard_map/enter/pallas_call | solution.py:118
  4.0 0.0 copy-start.2
  4.0 5.1 %collective-permute-start = (bf16[4,4,4,512]{3,2,1,0:T(4,128)(2,1)}, bf16[4,4,4,512]{3,2,1,0:T(4,128)(2,1)S(1)}, u32[]{:S(2)}, u32[]{:S(2)}) collective-permute-start(bf16[4,4,4,512]{3,2,1,0:T(4,128)(2,1)} %get-tuple-element.8), channel_id=1, source_target_pairs={{0,1},{1,0},{2,3},{3,2},{4,5},{5,4},{6,7},{7,6},{8,9},{9,8},{10,11... | collective-permute-start | bytes 196616 | tf_op jit(solution)/shard_map/ppermute | solution.py:28
  9.1 6.2 %all-to-all-start = ((bf16[16,16,2048]{2,1,0:T(8,128)(2,1)}), bf16[16,16,2048]{2,1,0:T(8,128)(2,1)S(1)}, u32[]{:S(2)}, u32[]{:S(2)}) async-start(bf16[16,16,2048]{2,1,0:T(8,128)(2,1)} %bitcast.98), calls=%async_computation | async-start | bytes 2097152 | tf_op jit(solution)/shard_map/all_to_all | solution.py:21
  15.4 0.0 collective-permute-done
  15.4 3.9 %collective-permute-start.2 = (bf16[2,4,4,512]{3,2,0,1:T(4,128)(2,1)S(1)}, bf16[2,4,4,512]{3,2,0,1:T(4,128)(2,1)S(1)}, u32[]{:S(2)}, u32[]{:S(2)}) collective-permute-start(bf16[2,4,4,512]{3,2,0,1:T(4,128)(2,1)S(1)} %pad_maximum_fusion.1), channel_id=1, source_target_pairs={{0,4},{1,5},{2,6},{3,7},{4,0},{5,1},{6,2},{7,3},{8,12},{9,13},{10,... | collective-permute-start | bytes 98312 | tf_op jit(solution)/shard_map/ppermute | solution.py:28
  19.4 3.8 %collective-permute-start.1 = (bf16[2,4,4,512]{3,2,0,1:T(4,128)(2,1)S(1)}, bf16[2,4,4,512]{3,2,0,1:T(4,128)(2,1)S(1)}, u32[]{:S(2)}, u32[]{:S(2)}) collective-permute-start(bf16[2,4,4,512]{3,2,0,1:T(4,128)(2,1)S(1)} %pad_maximum_fusion), channel_id=1, source_target_pairs={{0,2},{1,3},{2,0},{3,1},{4,6},{5,7},{6,4},{7,5},{8,10},{9,11},{10,... | collective-permute-start | bytes 98312 | tf_op jit(solution)/shard_map/ppermute | solution.py:28
  23.3 2.4 %collective-permute-start.3 = (bf16[2,4,4,512]{3,2,1,0:T(4,128)(2,1)S(1)}, bf16[2,4,4,512]{3,2,1,0:T(4,128)(2,1)S(1)}, u32[]{:S(2)}, u32[]{:S(2)}) collective-permute-start(bf16[2,4,4,512]{3,2,1,0:T(4,128)(2,1)S(1)} %pad_maximum_fusion.2), channel_id=1, source_target_pairs={{0,6},{1,7},{2,4},{3,5},{4,2},{5,3},{6,0},{7,1},{8,14},{9,15},{10,... | collective-permute-start | bytes 98312 | tf_op jit(solution)/shard_map/ppermute | solution.py:28
  25.8 5.2 %collective-permute-done.3 = bf16[2,4,4,512]{3,2,1,0:T(4,128)(2,1)S(1)} collective-permute-done((bf16[2,4,4,512]{3,2,1,0:T(4,128)(2,1)S(1)}, bf16[2,4,4,512]{3,2,1,0:T(4,128)(2,1)S(1)}, u32[]{:S(2)}, u32[]{:S(2)}) %collective-permute-start.3) | collective-permute-done | bytes 32800 | tf_op jit(solution)/shard_map/ppermute | solution.py:28
  30.9 0.0 all-to-all-done.spread_ref
  30.9 1.7 %pick.1 = bf16[16,16,2048]{2,1,0:T(8,128)(2,1)} custom-call(s32[16]{0:T(128)S(1)} %copy-done, bf16[16,16,2048]{2,1,0:T(8,128)(2,1)S(1)} %all-to-all-done.spread_ref), custom_call_target="tpu_custom_call" | custom-call | flops 1000000 | bytes 2000000 | tf_op jit(solution)/shard_map/pick/pallas_call | solution.py:148
  32.6 5.7 %all-to-all-start.1 = ((bf16[16,16,2048]{2,1,0:T(8,128)(2,1)}), bf16[16,16,2048]{2,1,0:T(8,128)(2,1)}, u32[]{:S(2)}, u32[]{:S(2)}) async-start(bf16[16,16,2048]{2,1,0:T(8,128)(2,1)} %pick.1), calls=%async_computation.1 | async-start | bytes 2097152 | tf_op jit(solution)/shard_map/all_to_all | solution.py:21
  38.4 9.1 %collective-permute-start.4 = (bf16[4,2,4,512]{3,2,1,0:T(4,128)(2,1)S(1)}, bf16[4,2,4,512]{3,2,1,0:T(4,128)(2,1)S(1)}, u32[]{:S(2)}, u32[]{:S(2)}) collective-permute-start(bf16[4,2,4,512]{3,2,1,0:T(4,128)(2,1)S(1)} %pad_maximum_fusion.3), channel_id=1, source_target_pairs={{0,8},{1,9},{2,10},{3,11},{4,12},{5,13},{6,14},{7,15},{8,0},{9,1},... | collective-permute-start | bytes 98312 | tf_op jit(solution)/shard_map/ppermute | solution.py:28
  47.5 9.0 %collective-permute-start.5 = (bf16[4,2,4,512]{3,2,1,0:T(4,128)(2,1)S(1)}, bf16[4,2,4,512]{3,2,1,0:T(4,128)(2,1)S(1)}, u32[]{:S(2)}, u32[]{:S(2)}) collective-permute-start(bf16[4,2,4,512]{3,2,1,0:T(4,128)(2,1)S(1)} %pad_maximum_fusion.4), channel_id=1, source_target_pairs={{0,16},{1,17},{2,18},{3,19},{4,20},{5,21},{6,22},{7,23},{8,24},{9,... | collective-permute-start | bytes 98312 | tf_op jit(solution)/shard_map/ppermute | solution.py:28
  56.5 1.9 %collective-permute-start.6 = (bf16[4,2,4,512]{3,2,1,0:T(4,128)(2,1)S(1)}, bf16[4,2,4,512]{3,2,1,0:T(4,128)(2,1)S(1)}, u32[]{:S(2)}, u32[]{:S(2)}) collective-permute-start(bf16[4,2,4,512]{3,2,1,0:T(4,128)(2,1)S(1)} %pad_maximum_fusion.5), channel_id=1, source_target_pairs={{0,24},{1,25},{2,26},{3,27},{4,28},{5,29},{6,30},{7,31},{8,16},{9,... | collective-permute-start | bytes 98312 | tf_op jit(solution)/shard_map/ppermute | solution.py:28
  58.5 0.0 all-to-all-done.1
  58.5 12.0 %all-to-all-start.2 = ((bf16[32,8,2048]{2,1,0:T(8,128)(2,1)}), bf16[32,8,2048]{2,1,0:T(8,128)(2,1)S(1)}, u32[]{:S(2)}, u32[]{:S(2)}) async-start(bf16[32,8,2048]{2,1,0:T(8,128)(2,1)} %bitcast.19.routed_ref), calls=%async_computation.2 | async-start | bytes 2097152 | tf_op jit(solution)/shard_map/all_to_all | solution.py:21
  70.6 0.0 copy-start.4
  70.6 0.0 copy-start.3
  70.6 0.0 copy-start.1
  70.6 0.0 collective-permute-done.4
  70.6 0.0 collective-permute-done.5
  70.7 0.0 collective-permute-done.6
  70.7 2.8 %multiply.1 = (f32[8,2,16,256]{3,2,1,0:T(8,128)S(1)}, f32[8,2,16,256]{3,2,1,0:T(8,128)S(1)}) custom-call(s32[1]{0:T(128)} %bitcast.me_ref, bf16[32,4,512]{2,1,0:T(4,128)(2,1)S(1)} %bitcast.96, bf16[32,8,2048]{2,1,0:T(8,128)(2,1)} %bitcast.19.routed_ref), custom_call_target="tpu_custom_call" | custom-call | flops 134217728 | bytes 3000000 | tf_op jit(solution)/shard_map/multiply/pallas_call | solution.py:197
  73.6 5.2 %collective-permute-start.7 = (f32[8,2,16,256]{3,2,1,0:T(8,128)S(1)}, f32[8,2,16,256]{3,2,1,0:T(8,128)S(1)}, u32[]{:S(2)}, u32[]{:S(2)}) collective-permute-start(f32[8,2,16,256]{3,2,1,0:T(8,128)S(1)} %get-tuple-element.11), channel_id=1, source_target_pairs={{0,1},{1,0},{2,3},{3,2},{4,5},{5,4},{6,7},{7,6},{8,9},{9,8},{10,11... | collective-permute-start | bytes 786440 | tf_op jit(solution)/shard_map/ppermute | solution.py:215
  78.8 7.5 %collective-permute-done.7 = f32[8,2,16,256]{3,2,1,0:T(8,128)S(1)} collective-permute-done((f32[8,2,16,256]{3,2,1,0:T(8,128)S(1)}, f32[8,2,16,256]{3,2,1,0:T(8,128)S(1)}, u32[]{:S(2)}, u32[]{:S(2)}) %collective-permute-start.7) | collective-permute-done | bytes 262176 | tf_op jit(solution)/shard_map/ppermute | solution.py:215
  86.4 9.0 %collective-permute-start.10 = (bf16[2,16,384]{2,1,0:T(8,128)(2,1)S(1)}, bf16[2,16,384]{2,1,0:T(8,128)(2,1)S(1)}, u32[]{:S(2)}, u32[]{:S(2)}) collective-permute-start(bf16[2,16,384]{2,1,0:T(8,128)(2,1)S(1)} %get-tuple-element.16), channel_id=1, source_target_pairs={{0,12},{1,13},{2,14},{3,15},{4,8},{5,9},{6,10},{7,11},{8,4},{9,5},... | collective-permute-start | bytes 73736 | tf_op jit(solution)/shard_map/ppermute | solution.py:215
  95.5 3.8 %collective-permute-start.11 = (bf16[2,16,384]{2,1,0:T(8,128)(2,1)S(1)}, bf16[2,16,384]{2,1,0:T(8,128)(2,1)S(1)}, u32[]{:S(2)}, u32[]{:S(2)}) collective-permute-start(bf16[2,16,384]{2,1,0:T(8,128)(2,1)S(1)} %get-tuple-element.17), channel_id=1, source_target_pairs={{0,24},{1,25},{2,26},{3,27},{4,28},{5,29},{6,30},{7,31},{8,16},{9,... | collective-permute-start | bytes 73736 | tf_op jit(solution)/shard_map/ppermute | solution.py:215
  99.3 0.1 dynamic_slice.3
  99.4 4.4 %collective-permute-start.12 = (bf16[2,16,384]{2,1,0:T(8,128)(2,1)S(1)}, bf16[2,16,384]{2,1,0:T(8,128)(2,1)S(1)}, u32[]{:S(2)}, u32[]{:S(2)}) collective-permute-start(bf16[2,16,384]{2,1,0:T(8,128)(2,1)S(1)} %get-tuple-element.18), channel_id=1, source_target_pairs={{0,8},{1,9},{2,10},{3,11},{4,12},{5,13},{6,14},{7,15},{8,0},{9,1},... | collective-permute-start | bytes 73736 | tf_op jit(solution)/shard_map/ppermute | solution.py:215
  103.9 2.2 %collective-permute-start.13 = (bf16[2,16,384]{2,1,0:T(8,128)(2,1)S(1)}, bf16[2,16,384]{2,1,0:T(8,128)(2,1)S(1)}, u32[]{:S(2)}, u32[]{:S(2)}) collective-permute-start(bf16[2,16,384]{2,1,0:T(8,128)(2,1)S(1)} %get-tuple-element.20), channel_id=1, source_target_pairs={{0,28},{1,29},{2,30},{3,31},{4,24},{5,25},{6,26},{7,27},{8,20},{9,... | collective-permute-start | bytes 73736 | tf_op jit(solution)/shard_map/ppermute | solution.py:215
  106.1 5.5 %collective-permute-start.14 = (bf16[2,16,384]{2,1,0:T(8,128)(2,1)S(1)}, bf16[2,16,384]{2,1,0:T(8,128)(2,1)S(1)}, u32[]{:S(2)}, u32[]{:S(2)}) collective-permute-start(bf16[2,16,384]{2,1,0:T(8,128)(2,1)S(1)} %get-tuple-element.19), channel_id=1, source_target_pairs={{0,4},{1,5},{2,6},{3,7},{4,0},{5,1},{6,2},{7,3},{8,12},{9,13},{10,... | collective-permute-start | bytes 73736 | tf_op jit(solution)/shard_map/ppermute | solution.py:215
  111.6 12.4 %collective-permute-done.10 = bf16[2,16,384]{2,1,0:T(8,128)(2,1)S(1)} collective-permute-done((bf16[2,16,384]{2,1,0:T(8,128)(2,1)S(1)}, bf16[2,16,384]{2,1,0:T(8,128)(2,1)S(1)}, u32[]{:S(2)}, u32[]{:S(2)}) %collective-permute-start.10) | collective-permute-done | bytes 24608 | tf_op jit(solution)/shard_map/ppermute | solution.py:215
  123.9 7.7 %collective-permute-start.8 = (bf16[2,16,384]{2,1,0:T(8,128)(2,1)S(1)}, bf16[2,16,384]{2,1,0:T(8,128)(2,1)S(1)}, u32[]{:S(2)}, u32[]{:S(2)}) collective-permute-start(bf16[2,16,384]{2,1,0:T(8,128)(2,1)S(1)} %get-tuple-element.14), channel_id=1, source_target_pairs={{0,16},{1,17},{2,18},{3,19},{4,20},{5,21},{6,22},{7,23},{8,24},{9,... | collective-permute-start | bytes 73736 | tf_op jit(solution)/shard_map/ppermute | solution.py:215
  131.7 2.5 %collective-permute-start.9 = (bf16[2,16,384]{2,1,0:T(8,128)(2,1)S(1)}, bf16[2,16,384]{2,1,0:T(8,128)(2,1)S(1)}, u32[]{:S(2)}, u32[]{:S(2)}) collective-permute-start(bf16[2,16,384]{2,1,0:T(8,128)(2,1)S(1)} %get-tuple-element.15), channel_id=1, source_target_pairs={{0,20},{1,21},{2,22},{3,23},{4,16},{5,17},{6,18},{7,19},{8,28},{9,... | collective-permute-start | bytes 73736 | tf_op jit(solution)/shard_map/ppermute | solution.py:215
  134.2 0.1 iota_compare_fusion
  134.3 0.0 collective-permute-done.12
  134.3 0.0 collective-permute-done.14
  134.3 4.0 %collective-permute-done.8 = bf16[2,16,384]{2,1,0:T(8,128)(2,1)S(1)} collective-permute-done((bf16[2,16,384]{2,1,0:T(8,128)(2,1)S(1)}, bf16[2,16,384]{2,1,0:T(8,128)(2,1)S(1)}, u32[]{:S(2)}, u32[]{:S(2)}) %collective-permute-start.8) | collective-permute-done | bytes 24608 | tf_op jit(solution)/shard_map/ppermute | solution.py:215
  138.4 6.0 %collective-permute-done.9 = bf16[2,16,384]{2,1,0:T(8,128)(2,1)S(1)} collective-permute-done((bf16[2,16,384]{2,1,0:T(8,128)(2,1)S(1)}, bf16[2,16,384]{2,1,0:T(8,128)(2,1)S(1)}, u32[]{:S(2)}, u32[]{:S(2)}) %collective-permute-start.9) | collective-permute-done | bytes 24608 | tf_op jit(solution)/shard_map/ppermute | solution.py:215
  144.5 1.9 %collective-permute-start.15 = (f32[16,256]{1,0:T(8,128)S(1)}, f32[16,256]{1,0:T(8,128)S(1)}, u32[]{:S(2)}, u32[]{:S(2)}) collective-permute-start(f32[16,256]{1,0:T(8,128)S(1)} %slice_bitcast_fusion.1), channel_id=1, source_target_pairs={{0,2},{1,3},{2,0},{3,1},{4,6},{5,7},{6,4},{7,5},{8,10},{9,11},{10,... | collective-permute-start | bytes 49160 | tf_op jit(solution)/shard_map/ppermute | solution.py:215
  146.4 0.5 fusion.40
  146.9 3.2 %collective-permute-done.15 = f32[16,256]{1,0:T(8,128)S(1)} collective-permute-done((f32[16,256]{1,0:T(8,128)S(1)}, f32[16,256]{1,0:T(8,128)S(1)}, u32[]{:S(2)}, u32[]{:S(2)}) %collective-permute-start.15) | collective-permute-done | bytes 16416 | tf_op jit(solution)/shard_map/ppermute | solution.py:215
  150.1 0.1 fusion.30
  150.3 0.2 fusion.5
  150.5 0.3 fusion.1
  150.8 0.7 copy.33
  151.5 1.2 copy.17
  (44 shorter events, 0.6 us)
Async XLA Ops:
  0.6 30.3 %copy-start = (s32[16]{0:T(128)S(1)}, s32[16]{0:T(128)}, u32[]{:S(2)}) copy-start(s32[16]{0:T(128)} %group_ref.1) | copy-start | bytes 196
  4.0 11.3 %copy-start.2 = (bf16[4,4,4,512]{3,2,1,0:T(4,128)(2,1)S(1)}, bf16[4,4,4,512]{3,2,1,0:T(4,128)(2,1)}, u32[]{:S(2)}) copy-start(bf16[4,4,4,512]{3,2,1,0:T(4,128)(2,1)} %get-tuple-element.7) | copy-start | bytes 196612
  4.0 11.4 %collective-permute-start = (bf16[4,4,4,512]{3,2,1,0:T(4,128)(2,1)}, bf16[4,4,4,512]{3,2,1,0:T(4,128)(2,1)S(1)}, u32[]{:S(2)}, u32[]{:S(2)}) collective-permute-start(bf16[4,4,4,512]{3,2,1,0:T(4,128)(2,1)} %get-tuple-element.8), channel_id=1, source_target_pairs={{0,1},{1,0},{2,3},{3,2},{4,5},{5,4},{6,7},{7,6},{8,9},{9,8},{10,11... | collective-permute-start | bytes 196616 | tf_op jit(solution)/shard_map/ppermute | solution.py:28
  9.1 21.9 %all-to-all-start = ((bf16[16,16,2048]{2,1,0:T(8,128)(2,1)}), bf16[16,16,2048]{2,1,0:T(8,128)(2,1)S(1)}, u32[]{:S(2)}, u32[]{:S(2)}) async-start(bf16[16,16,2048]{2,1,0:T(8,128)(2,1)} %bitcast.98), calls=%async_computation | async-start | bytes 2097152 | tf_op jit(solution)/shard_map/all_to_all | solution.py:21
  15.4 10.3 %collective-permute-start.2 = (bf16[2,4,4,512]{3,2,0,1:T(4,128)(2,1)S(1)}, bf16[2,4,4,512]{3,2,0,1:T(4,128)(2,1)S(1)}, u32[]{:S(2)}, u32[]{:S(2)}) collective-permute-start(bf16[2,4,4,512]{3,2,0,1:T(4,128)(2,1)S(1)} %pad_maximum_fusion.1), channel_id=1, source_target_pairs={{0,4},{1,5},{2,6},{3,7},{4,0},{5,1},{6,2},{7,3},{8,12},{9,13},{10,... | collective-permute-start | bytes 98312 | tf_op jit(solution)/shard_map/ppermute | solution.py:28
  19.4 6.3 %collective-permute-start.1 = (bf16[2,4,4,512]{3,2,0,1:T(4,128)(2,1)S(1)}, bf16[2,4,4,512]{3,2,0,1:T(4,128)(2,1)S(1)}, u32[]{:S(2)}, u32[]{:S(2)}) collective-permute-start(bf16[2,4,4,512]{3,2,0,1:T(4,128)(2,1)S(1)} %pad_maximum_fusion), channel_id=1, source_target_pairs={{0,2},{1,3},{2,0},{3,1},{4,6},{5,7},{6,4},{7,5},{8,10},{9,11},{10,... | collective-permute-start | bytes 98312 | tf_op jit(solution)/shard_map/ppermute | solution.py:28
  23.3 7.6 %collective-permute-start.3 = (bf16[2,4,4,512]{3,2,1,0:T(4,128)(2,1)S(1)}, bf16[2,4,4,512]{3,2,1,0:T(4,128)(2,1)S(1)}, u32[]{:S(2)}, u32[]{:S(2)}) collective-permute-start(bf16[2,4,4,512]{3,2,1,0:T(4,128)(2,1)S(1)} %pad_maximum_fusion.2), channel_id=1, source_target_pairs={{0,6},{1,7},{2,4},{3,5},{4,2},{5,3},{6,0},{7,1},{8,14},{9,15},{10,... | collective-permute-start | bytes 98312 | tf_op jit(solution)/shard_map/ppermute | solution.py:28
  32.6 25.9 %all-to-all-start.1 = ((bf16[16,16,2048]{2,1,0:T(8,128)(2,1)}), bf16[16,16,2048]{2,1,0:T(8,128)(2,1)}, u32[]{:S(2)}, u32[]{:S(2)}) async-start(bf16[16,16,2048]{2,1,0:T(8,128)(2,1)} %pick.1), calls=%async_computation.1 | async-start | bytes 2097152 | tf_op jit(solution)/shard_map/all_to_all | solution.py:21
  38.4 32.3 %collective-permute-start.4 = (bf16[4,2,4,512]{3,2,1,0:T(4,128)(2,1)S(1)}, bf16[4,2,4,512]{3,2,1,0:T(4,128)(2,1)S(1)}, u32[]{:S(2)}, u32[]{:S(2)}) collective-permute-start(bf16[4,2,4,512]{3,2,1,0:T(4,128)(2,1)S(1)} %pad_maximum_fusion.3), channel_id=1, source_target_pairs={{0,8},{1,9},{2,10},{3,11},{4,12},{5,13},{6,14},{7,15},{8,0},{9,1},... | collective-permute-start | bytes 98312 | tf_op jit(solution)/shard_map/ppermute | solution.py:28
  47.5 23.1 %collective-permute-start.5 = (bf16[4,2,4,512]{3,2,1,0:T(4,128)(2,1)S(1)}, bf16[4,2,4,512]{3,2,1,0:T(4,128)(2,1)S(1)}, u32[]{:S(2)}, u32[]{:S(2)}) collective-permute-start(bf16[4,2,4,512]{3,2,1,0:T(4,128)(2,1)S(1)} %pad_maximum_fusion.4), channel_id=1, source_target_pairs={{0,16},{1,17},{2,18},{3,19},{4,20},{5,21},{6,22},{7,23},{8,24},{9,... | collective-permute-start | bytes 98312 | tf_op jit(solution)/shard_map/ppermute | solution.py:28
  56.5 14.1 %collective-permute-start.6 = (bf16[4,2,4,512]{3,2,1,0:T(4,128)(2,1)S(1)}, bf16[4,2,4,512]{3,2,1,0:T(4,128)(2,1)S(1)}, u32[]{:S(2)}, u32[]{:S(2)}) collective-permute-start(bf16[4,2,4,512]{3,2,1,0:T(4,128)(2,1)S(1)} %pad_maximum_fusion.5), channel_id=1, source_target_pairs={{0,24},{1,25},{2,26},{3,27},{4,28},{5,29},{6,30},{7,31},{8,16},{9,... | collective-permute-start | bytes 98312 | tf_op jit(solution)/shard_map/ppermute | solution.py:28
  58.5 92.9 %all-to-all-start.2 = ((bf16[32,8,2048]{2,1,0:T(8,128)(2,1)}), bf16[32,8,2048]{2,1,0:T(8,128)(2,1)S(1)}, u32[]{:S(2)}, u32[]{:S(2)}) async-start(bf16[32,8,2048]{2,1,0:T(8,128)(2,1)} %bitcast.19.routed_ref), calls=%async_computation.2 | async-start | bytes 2097152 | tf_op jit(solution)/shard_map/all_to_all | solution.py:21
  70.6 28.7 %copy-start.4 = (s32[128]{0:T(128)S(1)}, s32[128]{0:T(128)}, u32[]{:S(2)}) copy-start(s32[128]{0:T(128)} %param.11) | copy-start | bytes 1540
  70.6 63.7 %copy-start.3 = (bf16[16,2048]{1,0:T(8,128)(2,1)S(1)}, bf16[16,2048]{1,0:T(8,128)(2,1)}, u32[]{:S(2)}) copy-start(bf16[16,2048]{1,0:T(8,128)(2,1)} %param.9) | copy-start | bytes 196612
  70.6 75.8 %copy-start.1 = (bf16[16,128,256]{2,1,0:T(8,128)(2,1)S(1)}, bf16[16,128,256]{2,1,0:T(8,128)(2,1)}, u32[]{:S(2)}) copy-start(bf16[16,128,256]{2,1,0:T(8,128)(2,1)} %param.10) | copy-start | bytes 3145732
  73.6 12.8 %collective-permute-start.7 = (f32[8,2,16,256]{3,2,1,0:T(8,128)S(1)}, f32[8,2,16,256]{3,2,1,0:T(8,128)S(1)}, u32[]{:S(2)}, u32[]{:S(2)}) collective-permute-start(f32[8,2,16,256]{3,2,1,0:T(8,128)S(1)} %get-tuple-element.11), channel_id=1, source_target_pairs={{0,1},{1,0},{2,3},{3,2},{4,5},{5,4},{6,7},{7,6},{8,9},{9,8},{10,11... | collective-permute-start | bytes 786440 | tf_op jit(solution)/shard_map/ppermute | solution.py:215
  86.4 37.5 %collective-permute-start.10 = (bf16[2,16,384]{2,1,0:T(8,128)(2,1)S(1)}, bf16[2,16,384]{2,1,0:T(8,128)(2,1)S(1)}, u32[]{:S(2)}, u32[]{:S(2)}) collective-permute-start(bf16[2,16,384]{2,1,0:T(8,128)(2,1)S(1)} %get-tuple-element.16), channel_id=1, source_target_pairs={{0,12},{1,13},{2,14},{3,15},{4,8},{5,9},{6,10},{7,11},{8,4},{9,5},... | collective-permute-start | bytes 73736 | tf_op jit(solution)/shard_map/ppermute | solution.py:215
  95.5 36.2 %collective-permute-start.11 = (bf16[2,16,384]{2,1,0:T(8,128)(2,1)S(1)}, bf16[2,16,384]{2,1,0:T(8,128)(2,1)S(1)}, u32[]{:S(2)}, u32[]{:S(2)}) collective-permute-start(bf16[2,16,384]{2,1,0:T(8,128)(2,1)S(1)} %get-tuple-element.17), channel_id=1, source_target_pairs={{0,24},{1,25},{2,26},{3,27},{4,28},{5,29},{6,30},{7,31},{8,16},{9,... | collective-permute-start | bytes 73736 | tf_op jit(solution)/shard_map/ppermute | solution.py:215
  99.4 34.9 %collective-permute-start.12 = (bf16[2,16,384]{2,1,0:T(8,128)(2,1)S(1)}, bf16[2,16,384]{2,1,0:T(8,128)(2,1)S(1)}, u32[]{:S(2)}, u32[]{:S(2)}) collective-permute-start(bf16[2,16,384]{2,1,0:T(8,128)(2,1)S(1)} %get-tuple-element.18), channel_id=1, source_target_pairs={{0,8},{1,9},{2,10},{3,11},{4,12},{5,13},{6,14},{7,15},{8,0},{9,1},... | collective-permute-start | bytes 73736 | tf_op jit(solution)/shard_map/ppermute | solution.py:215
  103.9 30.5 %collective-permute-start.13 = (bf16[2,16,384]{2,1,0:T(8,128)(2,1)S(1)}, bf16[2,16,384]{2,1,0:T(8,128)(2,1)S(1)}, u32[]{:S(2)}, u32[]{:S(2)}) collective-permute-start(bf16[2,16,384]{2,1,0:T(8,128)(2,1)S(1)} %get-tuple-element.20), channel_id=1, source_target_pairs={{0,28},{1,29},{2,30},{3,31},{4,24},{5,25},{6,26},{7,27},{8,20},{9,... | collective-permute-start | bytes 73736 | tf_op jit(solution)/shard_map/ppermute | solution.py:215
  106.1 28.3 %collective-permute-start.14 = (bf16[2,16,384]{2,1,0:T(8,128)(2,1)S(1)}, bf16[2,16,384]{2,1,0:T(8,128)(2,1)S(1)}, u32[]{:S(2)}, u32[]{:S(2)}) collective-permute-start(bf16[2,16,384]{2,1,0:T(8,128)(2,1)S(1)} %get-tuple-element.19), channel_id=1, source_target_pairs={{0,4},{1,5},{2,6},{3,7},{4,0},{5,1},{6,2},{7,3},{8,12},{9,13},{10,... | collective-permute-start | bytes 73736 | tf_op jit(solution)/shard_map/ppermute | solution.py:215
  123.9 14.4 %collective-permute-start.8 = (bf16[2,16,384]{2,1,0:T(8,128)(2,1)S(1)}, bf16[2,16,384]{2,1,0:T(8,128)(2,1)S(1)}, u32[]{:S(2)}, u32[]{:S(2)}) collective-permute-start(bf16[2,16,384]{2,1,0:T(8,128)(2,1)S(1)} %get-tuple-element.14), channel_id=1, source_target_pairs={{0,16},{1,17},{2,18},{3,19},{4,20},{5,21},{6,22},{7,23},{8,24},{9,... | collective-permute-start | bytes 73736 | tf_op jit(solution)/shard_map/ppermute | solution.py:215
  131.7 12.7 %collective-permute-start.9 = (bf16[2,16,384]{2,1,0:T(8,128)(2,1)S(1)}, bf16[2,16,384]{2,1,0:T(8,128)(2,1)S(1)}, u32[]{:S(2)}, u32[]{:S(2)}) collective-permute-start(bf16[2,16,384]{2,1,0:T(8,128)(2,1)S(1)} %get-tuple-element.15), channel_id=1, source_target_pairs={{0,20},{1,21},{2,22},{3,23},{4,16},{5,17},{6,18},{7,19},{8,28},{9,... | collective-permute-start | bytes 73736 | tf_op jit(solution)/shard_map/ppermute | solution.py:215
  144.5 5.6 %collective-permute-start.15 = (f32[16,256]{1,0:T(8,128)S(1)}, f32[16,256]{1,0:T(8,128)S(1)}, u32[]{:S(2)}, u32[]{:S(2)}) collective-permute-start(f32[16,256]{1,0:T(8,128)S(1)} %slice_bitcast_fusion.1), channel_id=1, source_target_pairs={{0,2},{1,3},{2,0},{3,1},{4,6},{5,7},{6,4},{7,5},{8,10},{9,11},{10,... | collective-permute-start | bytes 49160 | tf_op jit(solution)/shard_map/ppermute | solution.py:215

commit v2 on v0

--- a/solution.py
+++ b/solution.py
@@ -31,7 +31,7 @@
     near = [jnp.stack([v[k] for v in side]) for k in range(4)]
     near = [near[0]] + [send(near[k], k << 1) for k in range(1, 4)]
     far = [jnp.stack([v[:, k] for v in near]) for k in range(4)]
-    for k in (2, 1, 3):
+    for k in (1, 2, 3):
         far[k] = send(far[k], k << 3)
     return jnp.concatenate(far).reshape((shards,) + keep.shape[2:])
 
@@ -211,10 +211,7 @@
     halves = jnp.concatenate([head, rest], axis=-1).astype(jnp.bfloat16)
     arrived = {}
     for k in (4, 5, 3, 6, 2, 7, 1):
-        if k == 4:
-            arrived[k] = send(halves[k - 1, ::-1], 9 << 1)
-        else:
-            arrived[k] = send(halves[k - 1], k << 2)
+        arrived[k] = send(halves[k - 1], k << 2)
     total = sum(v.astype(jnp.float32) for v in arrived.values())
     keys = total[:, :, :HD] + total[:, :, 2 * HD :]
     partial = partial[0] + jnp.concatenate([keys, total[:, :, HD : 2 * HD]], axis=-1)

time: 175 us -> 169 us (0.966)
  the two profiles are of different devices: /device:TPU:32 before, /device:TPU:24 now
where the time goes in v2:
time: 169 us; the launch traced here: 168 us
  starting transfers between devices  102 us (60%)
  waiting for transfers between devices  54.7 us (32%)
  Pallas kernels  6.79 us (4%)
  local copies, waits for them, and re-layouts  2.15 us (1%)
    ppermute x16, starting transfers between devices, send(): return lax.ppermute(values, 'shard', [(i, i ^ bits) for i in range(shards)])  77.8 us
    ppermute x16, waiting for transfers between devices, send(): return lax.ppermute(values, 'shard', [(i, i ^ bits) for i in range(shards)])  40.4 us
    all_to_all x3, starting transfers between devices, exchange(): return lax.all_to_all(blocks, axis, split_axis=0, concat_axis=0, tiled=True)  23.8 us
    all_to_all x3, waiting for transfers between devices, exchange(): return lax.all_to_all(blocks, axis, split_axis=0, concat_axis=0, tiled=True)  14.4 us
  transfers between devices with their start and end apart: 19, of which 8 were waited for; matrix products, arithmetic and copies ran while one was open for 2% of the time, Pallas kernels for 2%

profile of v2, /device:TPU:24, one launch (start us, length us, event | category | flops | bytes accessed | tf_op | source)
XLA Modules:
  0.0 168.0 jit_solution(13753434205162121495)
XLA Ops:
  0.6 3.3 %enter.1 = (bf16[32,8,2048]{2,1,0:T(8,128)(2,1)}, bf16[4,4,4,512]{3,2,1,0:T(4,128)(2,1)}, bf16[4,4,4,512]{3,2,1,0:T(4,128)(2,1)}) custom-call(s32[1]{0:T(128)} %bitcast.me_ref, f32[1,512,1024]{2,1,0:T(8,128)} %weights_ref.1, bf16[4,16384]{1,0:T(4,128)(2,1)} %hidden_ref.1), custom_call_target="tpu_custom_call" | custom-call | flops 2000000 | bytes 3000000 | tf_op jit(solution)/shard_map/enter/pallas_call | solution.py:118
  4.0 0.0 copy-start.2
  4.0 5.1 %collective-permute-start = (bf16[4,4,4,512]{3,2,1,0:T(4,128)(2,1)}, bf16[4,4,4,512]{3,2,1,0:T(4,128)(2,1)S(1)}, u32[]{:S(2)}, u32[]{:S(2)}) collective-permute-start(bf16[4,4,4,512]{3,2,1,0:T(4,128)(2,1)} %get-tuple-element.6), channel_id=1, source_target_pairs={{0,1},{1,0},{2,3},{3,2},{4,5},{5,4},{6,7},{7,6},{8,9},{9,8},{10,11... | collective-permute-start | bytes 196616 | tf_op jit(solution)/shard_map/ppermute | solution.py:28
  9.1 6.0 %all-to-all-start = ((bf16[16,16,2048]{2,1,0:T(8,128)(2,1)}), bf16[16,16,2048]{2,1,0:T(8,128)(2,1)S(1)}, u32[]{:S(2)}, u32[]{:S(2)}) async-start(bf16[16,16,2048]{2,1,0:T(8,128)(2,1)} %bitcast.104), calls=%async_computation | async-start | bytes 2097152 | tf_op jit(solution)/shard_map/all_to_all | solution.py:21
  15.2 0.0 collective-permute-done
  15.3 3.9 %collective-permute-start.2 = (bf16[2,4,4,512]{3,2,0,1:T(4,128)(2,1)S(1)}, bf16[2,4,4,512]{3,2,0,1:T(4,128)(2,1)S(1)}, u32[]{:S(2)}, u32[]{:S(2)}) collective-permute-start(bf16[2,4,4,512]{3,2,0,1:T(4,128)(2,1)S(1)} %pad_maximum_fusion.1), channel_id=1, source_target_pairs={{0,4},{1,5},{2,6},{3,7},{4,0},{5,1},{6,2},{7,3},{8,12},{9,13},{10,... | collective-permute-start | bytes 98312 | tf_op jit(solution)/shard_map/ppermute | solution.py:28
  19.2 3.8 %collective-permute-start.1 = (bf16[2,4,4,512]{3,2,0,1:T(4,128)(2,1)S(1)}, bf16[2,4,4,512]{3,2,0,1:T(4,128)(2,1)S(1)}, u32[]{:S(2)}, u32[]{:S(2)}) collective-permute-start(bf16[2,4,4,512]{3,2,0,1:T(4,128)(2,1)S(1)} %pad_maximum_fusion), channel_id=1, source_target_pairs={{0,2},{1,3},{2,0},{3,1},{4,6},{5,7},{6,4},{7,5},{8,10},{9,11},{10,... | collective-permute-start | bytes 98312 | tf_op jit(solution)/shard_map/ppermute | solution.py:28
  23.1 2.4 %collective-permute-start.3 = (bf16[2,4,4,512]{3,2,1,0:T(4,128)(2,1)S(1)}, bf16[2,4,4,512]{3,2,1,0:T(4,128)(2,1)S(1)}, u32[]{:S(2)}, u32[]{:S(2)}) collective-permute-start(bf16[2,4,4,512]{3,2,1,0:T(4,128)(2,1)S(1)} %pad_maximum_fusion.2), channel_id=1, source_target_pairs={{0,6},{1,7},{2,4},{3,5},{4,2},{5,3},{6,0},{7,1},{8,14},{9,15},{10,... | collective-permute-start | bytes 98312 | tf_op jit(solution)/shard_map/ppermute | solution.py:28
  25.5 0.0 collective-permute-done.2
  25.5 0.0 collective-permute-done.1
  25.6 5.1 %collective-permute-done.3 = bf16[2,4,4,512]{3,2,1,0:T(4,128)(2,1)S(1)} collective-permute-done((bf16[2,4,4,512]{3,2,1,0:T(4,128)(2,1)S(1)}, bf16[2,4,4,512]{3,2,1,0:T(4,128)(2,1)S(1)}, u32[]{:S(2)}, u32[]{:S(2)}) %collective-permute-start.3) | collective-permute-done | bytes 32800 | tf_op jit(solution)/shard_map/ppermute | solution.py:28
  30.7 9.1 %collective-permute-start.4 = (bf16[4,2,4,512]{3,2,1,0:T(4,128)(2,1)S(1)}, bf16[4,2,4,512]{3,2,1,0:T(4,128)(2,1)S(1)}, u32[]{:S(2)}, u32[]{:S(2)}) collective-permute-start(bf16[4,2,4,512]{3,2,1,0:T(4,128)(2,1)S(1)} %pad_maximum_fusion.3), channel_id=1, source_target_pairs={{0,8},{1,9},{2,10},{3,11},{4,12},{5,13},{6,14},{7,15},{8,0},{9,1},... | collective-permute-start | bytes 98312 | tf_op jit(solution)/shard_map/ppermute | solution.py:28
  39.9 8.2 %collective-permute-start.5 = (bf16[4,2,4,512]{3,2,1,0:T(4,128)(2,1)S(1)}, bf16[4,2,4,512]{3,2,1,0:T(4,128)(2,1)S(1)}, u32[]{:S(2)}, u32[]{:S(2)}) collective-permute-start(bf16[4,2,4,512]{3,2,1,0:T(4,128)(2,1)S(1)} %pad_maximum_fusion.4), channel_id=1, source_target_pairs={{0,16},{1,17},{2,18},{3,19},{4,20},{5,21},{6,22},{7,23},{8,24},{9,... | collective-permute-start | bytes 98312 | tf_op jit(solution)/shard_map/ppermute | solution.py:28
  48.2 1.9 %collective-permute-start.6 = (bf16[4,2,4,512]{3,2,1,0:T(4,128)(2,1)S(1)}, bf16[4,2,4,512]{3,2,1,0:T(4,128)(2,1)S(1)}, u32[]{:S(2)}, u32[]{:S(2)}) collective-permute-start(bf16[4,2,4,512]{3,2,1,0:T(4,128)(2,1)S(1)} %pad_maximum_fusion.5), channel_id=1, source_target_pairs={{0,24},{1,25},{2,26},{3,27},{4,28},{5,29},{6,30},{7,31},{8,16},{9,... | collective-permute-start | bytes 98312 | tf_op jit(solution)/shard_map/ppermute | solution.py:28
  50.1 0.0 all-to-all-done.spread_ref
  50.1 1.7 pick.1
  51.8 5.7 %all-to-all-start.1 = ((bf16[16,16,2048]{2,1,0:T(8,128)(2,1)}), bf16[16,16,2048]{2,1,0:T(8,128)(2,1)}, u32[]{:S(2)}, u32[]{:S(2)}) async-start(bf16[16,16,2048]{2,1,0:T(8,128)(2,1)} %pick.1), calls=%async_computation.1 | async-start | bytes 2097152 | tf_op jit(solution)/shard_map/all_to_all | solution.py:21
  57.5 0.0 collective-permute-done.4
  57.6 0.3 collective-permute-done.6
  57.9 14.4 %all-to-all-done.1 = bf16[16,16,2048]{2,1,0:T(8,128)(2,1)} async-done(((bf16[16,16,2048]{2,1,0:T(8,128)(2,1)}), bf16[16,16,2048]{2,1,0:T(8,128)(2,1)}, u32[]{:S(2)}, u32[]{:S(2)}) %all-to-all-start.1) | async-done | bytes 1048608 | tf_op jit(solution)/shard_map/all_to_all | solution.py:21
  72.3 12.0 %all-to-all-start.2 = ((bf16[32,8,2048]{2,1,0:T(8,128)(2,1)}), bf16[32,8,2048]{2,1,0:T(8,128)(2,1)S(1)}, u32[]{:S(2)}, u32[]{:S(2)}) async-start(bf16[32,8,2048]{2,1,0:T(8,128)(2,1)} %bitcast.19.routed_ref), calls=%async_computation.2 | async-start | bytes 2097152 | tf_op jit(solution)/shard_map/all_to_all | solution.py:21
  84.3 0.0 copy-start.4
  84.3 0.0 copy-start.3
  84.3 0.0 copy-start.1
  84.3 1.8 %multiply.1 = f32[2,8,2,16,256]{4,3,2,1,0:T(8,128)S(1)} custom-call(s32[1]{0:T(128)} %bitcast.me_ref, bf16[32,4,512]{2,1,0:T(4,128)(2,1)S(1)} %bitcast.102, bf16[32,8,2048]{2,1,0:T(8,128)(2,1)} %bitcast.19.routed_ref), custom_call_target="tpu_custom_call" | custom-call | flops 134217728 | bytes 3000000 | tf_op jit(solution)/shard_map/multiply/pallas_call | solution.py:188
  86.2 5.2 %collective-permute-start.7 = (f32[8,2,16,256]{3,2,1,0:T(8,128)S(1)}, f32[8,2,16,256]{3,2,1,0:T(8,128)S(1)}, u32[]{:S(2)}, u32[]{:S(2)}) collective-permute-start(f32[8,2,16,256]{3,2,1,0:T(8,128)S(1)} %slice_bitcast_fusion), channel_id=1, source_target_pairs={{0,1},{1,0},{2,3},{3,2},{4,5},{5,4},{6,7},{7,6},{8,9},{9,8},{10,11... | collective-permute-start | bytes 786440 | tf_op jit(solution)/shard_map/ppermute | solution.py:206
  91.4 8.1 %collective-permute-done.7 = f32[8,2,16,256]{3,2,1,0:T(8,128)S(1)} collective-permute-done((f32[8,2,16,256]{3,2,1,0:T(8,128)S(1)}, f32[8,2,16,256]{3,2,1,0:T(8,128)S(1)}, u32[]{:S(2)}, u32[]{:S(2)}) %collective-permute-start.7) | collective-permute-done | bytes 262176 | tf_op jit(solution)/shard_map/ppermute | solution.py:206
  99.6 9.2 %collective-permute-start.10 = (bf16[2,16,384]{2,1,0:T(8,128)(2,1)S(1)}, bf16[2,16,384]{2,1,0:T(8,128)(2,1)S(1)}, u32[]{:S(2)}, u32[]{:S(2)}) collective-permute-start(bf16[2,16,384]{2,1,0:T(8,128)(2,1)S(1)} %get-tuple-element.12), channel_id=1, source_target_pairs={{0,12},{1,13},{2,14},{3,15},{4,8},{5,9},{6,10},{7,11},{8,4},{9,5},... | collective-permute-start | bytes 73736 | tf_op jit(solution)/shard_map/ppermute | solution.py:206
  108.8 4.4 %collective-permute-start.11 = (bf16[2,16,384]{2,1,0:T(8,128)(2,1)S(1)}, bf16[2,16,384]{2,1,0:T(8,128)(2,1)S(1)}, u32[]{:S(2)}, u32[]{:S(2)}) collective-permute-start(bf16[2,16,384]{2,1,0:T(8,128)(2,1)S(1)} %get-tuple-element.13), channel_id=1, source_target_pairs={{0,24},{1,25},{2,26},{3,27},{4,28},{5,29},{6,30},{7,31},{8,16},{9,... | collective-permute-start | bytes 73736 | tf_op jit(solution)/shard_map/ppermute | solution.py:206
  113.2 0.1 dynamic_slice.3
  113.3 3.8 %collective-permute-start.12 = (bf16[2,16,384]{2,1,0:T(8,128)(2,1)S(1)}, bf16[2,16,384]{2,1,0:T(8,128)(2,1)S(1)}, u32[]{:S(2)}, u32[]{:S(2)}) collective-permute-start(bf16[2,16,384]{2,1,0:T(8,128)(2,1)S(1)} %get-tuple-element.14), channel_id=1, source_target_pairs={{0,8},{1,9},{2,10},{3,11},{4,12},{5,13},{6,14},{7,15},{8,0},{9,1},... | collective-permute-start | bytes 73736 | tf_op jit(solution)/shard_map/ppermute | solution.py:206
  117.1 2.1 %collective-permute-start.13 = (bf16[2,16,384]{2,1,0:T(8,128)(2,1)S(1)}, bf16[2,16,384]{2,1,0:T(8,128)(2,1)S(1)}, u32[]{:S(2)}, u32[]{:S(2)}) collective-permute-start(bf16[2,16,384]{2,1,0:T(8,128)(2,1)S(1)} %get-tuple-element.16), channel_id=1, source_target_pairs={{0,28},{1,29},{2,30},{3,31},{4,24},{5,25},{6,26},{7,27},{8,20},{9,... | collective-permute-start | bytes 73736 | tf_op jit(solution)/shard_map/ppermute | solution.py:206
  119.2 5.6 %collective-permute-start.14 = (bf16[2,16,384]{2,1,0:T(8,128)(2,1)S(1)}, bf16[2,16,384]{2,1,0:T(8,128)(2,1)S(1)}, u32[]{:S(2)}, u32[]{:S(2)}) collective-permute-start(bf16[2,16,384]{2,1,0:T(8,128)(2,1)S(1)} %get-tuple-element.15), channel_id=1, source_target_pairs={{0,4},{1,5},{2,6},{3,7},{4,0},{5,1},{6,2},{7,3},{8,12},{9,13},{10,... | collective-permute-start | bytes 73736 | tf_op jit(solution)/shard_map/ppermute | solution.py:206
  124.8 13.0 %collective-permute-done.10 = bf16[2,16,384]{2,1,0:T(8,128)(2,1)S(1)} collective-permute-done((bf16[2,16,384]{2,1,0:T(8,128)(2,1)S(1)}, bf16[2,16,384]{2,1,0:T(8,128)(2,1)S(1)}, u32[]{:S(2)}, u32[]{:S(2)}) %collective-permute-start.10) | collective-permute-done | bytes 24608 | tf_op jit(solution)/shard_map/ppermute | solution.py:206
  137.9 9.3 %collective-permute-start.8 = (bf16[2,16,384]{2,1,0:T(8,128)(2,1)S(1)}, bf16[2,16,384]{2,1,0:T(8,128)(2,1)S(1)}, u32[]{:S(2)}, u32[]{:S(2)}) collective-permute-start(bf16[2,16,384]{2,1,0:T(8,128)(2,1)S(1)} %get-tuple-element.10), channel_id=1, source_target_pairs={{0,16},{1,17},{2,18},{3,19},{4,20},{5,21},{6,22},{7,23},{8,24},{9,... | collective-permute-start | bytes 73736 | tf_op jit(solution)/shard_map/ppermute | solution.py:206
  147.1 0.0 collective-permute-done.11
  147.2 1.9 %collective-permute-start.9 = (bf16[2,16,384]{2,1,0:T(8,128)(2,1)S(1)}, bf16[2,16,384]{2,1,0:T(8,128)(2,1)S(1)}, u32[]{:S(2)}, u32[]{:S(2)}) collective-permute-start(bf16[2,16,384]{2,1,0:T(8,128)(2,1)S(1)} %get-tuple-element.11), channel_id=1, source_target_pairs={{0,20},{1,21},{2,22},{3,23},{4,16},{5,17},{6,18},{7,19},{8,28},{9,... | collective-permute-start | bytes 73736 | tf_op jit(solution)/shard_map/ppermute | solution.py:206
  149.1 0.1 iota_compare_fusion
  149.2 3.1 %collective-permute-done.8 = bf16[2,16,384]{2,1,0:T(8,128)(2,1)S(1)} collective-permute-done((bf16[2,16,384]{2,1,0:T(8,128)(2,1)S(1)}, bf16[2,16,384]{2,1,0:T(8,128)(2,1)S(1)}, u32[]{:S(2)}, u32[]{:S(2)}) %collective-permute-start.8) | collective-permute-done | bytes 24608 | tf_op jit(solution)/shard_map/ppermute | solution.py:206
  152.3 7.5 %collective-permute-done.9 = bf16[2,16,384]{2,1,0:T(8,128)(2,1)S(1)} collective-permute-done((bf16[2,16,384]{2,1,0:T(8,128)(2,1)S(1)}, bf16[2,16,384]{2,1,0:T(8,128)(2,1)S(1)}, u32[]{:S(2)}, u32[]{:S(2)}) %collective-permute-start.9) | collective-permute-done | bytes 24608 | tf_op jit(solution)/shard_map/ppermute | solution.py:206
  159.9 1.9 %collective-permute-start.15 = (f32[16,256]{1,0:T(8,128)S(1)}, f32[16,256]{1,0:T(8,128)S(1)}, u32[]{:S(2)}, u32[]{:S(2)}) collective-permute-start(f32[16,256]{1,0:T(8,128)S(1)} %slice_bitcast_fusion.3), channel_id=1, source_target_pairs={{0,2},{1,3},{2,0},{3,1},{4,6},{5,7},{6,4},{7,5},{8,10},{9,11},{10,... | collective-permute-start | bytes 49160 | tf_op jit(solution)/shard_map/ppermute | solution.py:206
  161.8 0.5 fusion.41
  162.3 3.2 %collective-permute-done.15 = f32[16,256]{1,0:T(8,128)S(1)} collective-permute-done((f32[16,256]{1,0:T(8,128)S(1)}, f32[16,256]{1,0:T(8,128)S(1)}, u32[]{:S(2)}, u32[]{:S(2)}) %collective-permute-start.15) | collective-permute-done | bytes 16416 | tf_op jit(solution)/shard_map/ppermute | solution.py:206
  165.5 0.1 fusion.31
  165.7 0.2 fusion.6
  165.9 0.3 fusion.1
  166.2 0.7 copy.33
  166.9 1.2 copy.17
  (45 shorter events, 0.6 us)
Async XLA Ops:
  0.6 49.5 %copy-start = (s32[16]{0:T(128)S(1)}, s32[16]{0:T(128)}, u32[]{:S(2)}) copy-start(s32[16]{0:T(128)} %group_ref.1) | copy-start | bytes 196
  4.0 11.1 %copy-start.2 = (bf16[4,4,4,512]{3,2,1,0:T(4,128)(2,1)S(1)}, bf16[4,4,4,512]{3,2,1,0:T(4,128)(2,1)}, u32[]{:S(2)}) copy-start(bf16[4,4,4,512]{3,2,1,0:T(4,128)(2,1)} %get-tuple-element.5) | copy-start | bytes 196612
  4.0 11.2 %collective-permute-start = (bf16[4,4,4,512]{3,2,1,0:T(4,128)(2,1)}, bf16[4,4,4,512]{3,2,1,0:T(4,128)(2,1)S(1)}, u32[]{:S(2)}, u32[]{:S(2)}) collective-permute-start(bf16[4,4,4,512]{3,2,1,0:T(4,128)(2,1)} %get-tuple-element.6), channel_id=1, source_target_pairs={{0,1},{1,0},{2,3},{3,2},{4,5},{5,4},{6,7},{7,6},{8,9},{9,8},{10,11... | collective-permute-start | bytes 196616 | tf_op jit(solution)/shard_map/ppermute | solution.py:28
  9.1 41.0 %all-to-all-start = ((bf16[16,16,2048]{2,1,0:T(8,128)(2,1)}), bf16[16,16,2048]{2,1,0:T(8,128)(2,1)S(1)}, u32[]{:S(2)}, u32[]{:S(2)}) async-start(bf16[16,16,2048]{2,1,0:T(8,128)(2,1)} %bitcast.104), calls=%async_computation | async-start | bytes 2097152 | tf_op jit(solution)/shard_map/all_to_all | solution.py:21
  15.3 10.2 %collective-permute-start.2 = (bf16[2,4,4,512]{3,2,0,1:T(4,128)(2,1)S(1)}, bf16[2,4,4,512]{3,2,0,1:T(4,128)(2,1)S(1)}, u32[]{:S(2)}, u32[]{:S(2)}) collective-permute-start(bf16[2,4,4,512]{3,2,0,1:T(4,128)(2,1)S(1)} %pad_maximum_fusion.1), channel_id=1, source_target_pairs={{0,4},{1,5},{2,6},{3,7},{4,0},{5,1},{6,2},{7,3},{8,12},{9,13},{10,... | collective-permute-start | bytes 98312 | tf_op jit(solution)/shard_map/ppermute | solution.py:28
  19.2 6.3 %collective-permute-start.1 = (bf16[2,4,4,512]{3,2,0,1:T(4,128)(2,1)S(1)}, bf16[2,4,4,512]{3,2,0,1:T(4,128)(2,1)S(1)}, u32[]{:S(2)}, u32[]{:S(2)}) collective-permute-start(bf16[2,4,4,512]{3,2,0,1:T(4,128)(2,1)S(1)} %pad_maximum_fusion), channel_id=1, source_target_pairs={{0,2},{1,3},{2,0},{3,1},{4,6},{5,7},{6,4},{7,5},{8,10},{9,11},{10,... | collective-permute-start | bytes 98312 | tf_op jit(solution)/shard_map/ppermute | solution.py:28
  23.1 7.6 %collective-permute-start.3 = (bf16[2,4,4,512]{3,2,1,0:T(4,128)(2,1)S(1)}, bf16[2,4,4,512]{3,2,1,0:T(4,128)(2,1)S(1)}, u32[]{:S(2)}, u32[]{:S(2)}) collective-permute-start(bf16[2,4,4,512]{3,2,1,0:T(4,128)(2,1)S(1)} %pad_maximum_fusion.2), channel_id=1, source_target_pairs={{0,6},{1,7},{2,4},{3,5},{4,2},{5,3},{6,0},{7,1},{8,14},{9,15},{10,... | collective-permute-start | bytes 98312 | tf_op jit(solution)/shard_map/ppermute | solution.py:28
  30.7 26.8 %collective-permute-start.4 = (bf16[4,2,4,512]{3,2,1,0:T(4,128)(2,1)S(1)}, bf16[4,2,4,512]{3,2,1,0:T(4,128)(2,1)S(1)}, u32[]{:S(2)}, u32[]{:S(2)}) collective-permute-start(bf16[4,2,4,512]{3,2,1,0:T(4,128)(2,1)S(1)} %pad_maximum_fusion.3), channel_id=1, source_target_pairs={{0,8},{1,9},{2,10},{3,11},{4,12},{5,13},{6,14},{7,15},{8,0},{9,1},... | collective-permute-start | bytes 98312 | tf_op jit(solution)/shard_map/ppermute | solution.py:28
  39.9 17.7 %collective-permute-start.5 = (bf16[4,2,4,512]{3,2,1,0:T(4,128)(2,1)S(1)}, bf16[4,2,4,512]{3,2,1,0:T(4,128)(2,1)S(1)}, u32[]{:S(2)}, u32[]{:S(2)}) collective-permute-start(bf16[4,2,4,512]{3,2,1,0:T(4,128)(2,1)S(1)} %pad_maximum_fusion.4), channel_id=1, source_target_pairs={{0,16},{1,17},{2,18},{3,19},{4,20},{5,21},{6,22},{7,23},{8,24},{9,... | collective-permute-start | bytes 98312 | tf_op jit(solution)/shard_map/ppermute | solution.py:28
  48.2 9.7 %collective-permute-start.6 = (bf16[4,2,4,512]{3,2,1,0:T(4,128)(2,1)S(1)}, bf16[4,2,4,512]{3,2,1,0:T(4,128)(2,1)S(1)}, u32[]{:S(2)}, u32[]{:S(2)}) collective-permute-start(bf16[4,2,4,512]{3,2,1,0:T(4,128)(2,1)S(1)} %pad_maximum_fusion.5), channel_id=1, source_target_pairs={{0,24},{1,25},{2,26},{3,27},{4,28},{5,29},{6,30},{7,31},{8,16},{9,... | collective-permute-start | bytes 98312 | tf_op jit(solution)/shard_map/ppermute | solution.py:28
  51.8 20.5 %all-to-all-start.1 = ((bf16[16,16,2048]{2,1,0:T(8,128)(2,1)}), bf16[16,16,2048]{2,1,0:T(8,128)(2,1)}, u32[]{:S(2)}, u32[]{:S(2)}) async-start(bf16[16,16,2048]{2,1,0:T(8,128)(2,1)} %pick.1), calls=%async_computation.1 | async-start | bytes 2097152 | tf_op jit(solution)/shard_map/all_to_all | solution.py:21
  72.3 94.6 %all-to-all-start.2 = ((bf16[32,8,2048]{2,1,0:T(8,128)(2,1)}), bf16[32,8,2048]{2,1,0:T(8,128)(2,1)S(1)}, u32[]{:S(2)}, u32[]{:S(2)}) async-start(bf16[32,8,2048]{2,1,0:T(8,128)(2,1)} %bitcast.19.routed_ref), calls=%async_computation.2 | async-start | bytes 2097152 | tf_op jit(solution)/shard_map/all_to_all | solution.py:21
  84.3 28.9 %copy-start.4 = (s32[128]{0:T(128)S(1)}, s32[128]{0:T(128)}, u32[]{:S(2)}) copy-start(s32[128]{0:T(128)} %param.11) | copy-start | bytes 1540
  84.3 64.9 %copy-start.3 = (bf16[16,2048]{1,0:T(8,128)(2,1)S(1)}, bf16[16,2048]{1,0:T(8,128)(2,1)}, u32[]{:S(2)}) copy-start(bf16[16,2048]{1,0:T(8,128)(2,1)} %param.9) | copy-start | bytes 196612
  84.3 77.5 %copy-start.1 = (bf16[16,128,256]{2,1,0:T(8,128)(2,1)S(1)}, bf16[16,128,256]{2,1,0:T(8,128)(2,1)}, u32[]{:S(2)}) copy-start(bf16[16,128,256]{2,1,0:T(8,128)(2,1)} %param.10) | copy-start | bytes 3145732
  86.2 13.3 %collective-permute-start.7 = (f32[8,2,16,256]{3,2,1,0:T(8,128)S(1)}, f32[8,2,16,256]{3,2,1,0:T(8,128)S(1)}, u32[]{:S(2)}, u32[]{:S(2)}) collective-permute-start(f32[8,2,16,256]{3,2,1,0:T(8,128)S(1)} %slice_bitcast_fusion), channel_id=1, source_target_pairs={{0,1},{1,0},{2,3},{3,2},{4,5},{5,4},{6,7},{7,6},{8,9},{9,8},{10,11... | collective-permute-start | bytes 786440 | tf_op jit(solution)/shard_map/ppermute | solution.py:206
  99.6 38.3 %collective-permute-start.10 = (bf16[2,16,384]{2,1,0:T(8,128)(2,1)S(1)}, bf16[2,16,384]{2,1,0:T(8,128)(2,1)S(1)}, u32[]{:S(2)}, u32[]{:S(2)}) collective-permute-start(bf16[2,16,384]{2,1,0:T(8,128)(2,1)S(1)} %get-tuple-element.12), channel_id=1, source_target_pairs={{0,12},{1,13},{2,14},{3,15},{4,8},{5,9},{6,10},{7,11},{8,4},{9,5},... | collective-permute-start | bytes 73736 | tf_op jit(solution)/shard_map/ppermute | solution.py:206
  108.8 38.4 %collective-permute-start.11 = (bf16[2,16,384]{2,1,0:T(8,128)(2,1)S(1)}, bf16[2,16,384]{2,1,0:T(8,128)(2,1)S(1)}, u32[]{:S(2)}, u32[]{:S(2)}) collective-permute-start(bf16[2,16,384]{2,1,0:T(8,128)(2,1)S(1)} %get-tuple-element.13), channel_id=1, source_target_pairs={{0,24},{1,25},{2,26},{3,27},{4,28},{5,29},{6,30},{7,31},{8,16},{9,... | collective-permute-start | bytes 73736 | tf_op jit(solution)/shard_map/ppermute | solution.py:206
  113.3 35.9 %collective-permute-start.12 = (bf16[2,16,384]{2,1,0:T(8,128)(2,1)S(1)}, bf16[2,16,384]{2,1,0:T(8,128)(2,1)S(1)}, u32[]{:S(2)}, u32[]{:S(2)}) collective-permute-start(bf16[2,16,384]{2,1,0:T(8,128)(2,1)S(1)} %get-tuple-element.14), channel_id=1, source_target_pairs={{0,8},{1,9},{2,10},{3,11},{4,12},{5,13},{6,14},{7,15},{8,0},{9,1},... | collective-permute-start | bytes 73736 | tf_op jit(solution)/shard_map/ppermute | solution.py:206
  117.1 32.1 %collective-permute-start.13 = (bf16[2,16,384]{2,1,0:T(8,128)(2,1)S(1)}, bf16[2,16,384]{2,1,0:T(8,128)(2,1)S(1)}, u32[]{:S(2)}, u32[]{:S(2)}) collective-permute-start(bf16[2,16,384]{2,1,0:T(8,128)(2,1)S(1)} %get-tuple-element.16), channel_id=1, source_target_pairs={{0,28},{1,29},{2,30},{3,31},{4,24},{5,25},{6,26},{7,27},{8,20},{9,... | collective-permute-start | bytes 73736 | tf_op jit(solution)/shard_map/ppermute | solution.py:206
  119.2 30.0 %collective-permute-start.14 = (bf16[2,16,384]{2,1,0:T(8,128)(2,1)S(1)}, bf16[2,16,384]{2,1,0:T(8,128)(2,1)S(1)}, u32[]{:S(2)}, u32[]{:S(2)}) collective-permute-start(bf16[2,16,384]{2,1,0:T(8,128)(2,1)S(1)} %get-tuple-element.15), channel_id=1, source_target_pairs={{0,4},{1,5},{2,6},{3,7},{4,0},{5,1},{6,2},{7,3},{8,12},{9,13},{10,... | collective-permute-start | bytes 73736 | tf_op jit(solution)/shard_map/ppermute | solution.py:206
  137.9 14.4 %collective-permute-start.8 = (bf16[2,16,384]{2,1,0:T(8,128)(2,1)S(1)}, bf16[2,16,384]{2,1,0:T(8,128)(2,1)S(1)}, u32[]{:S(2)}, u32[]{:S(2)}) collective-permute-start(bf16[2,16,384]{2,1,0:T(8,128)(2,1)S(1)} %get-tuple-element.10), channel_id=1, source_target_pairs={{0,16},{1,17},{2,18},{3,19},{4,20},{5,21},{6,22},{7,23},{8,24},{9,... | collective-permute-start | bytes 73736 | tf_op jit(solution)/shard_map/ppermute | solution.py:206
  147.2 12.6 %collective-permute-start.9 = (bf16[2,16,384]{2,1,0:T(8,128)(2,1)S(1)}, bf16[2,16,384]{2,1,0:T(8,128)(2,1)S(1)}, u32[]{:S(2)}, u32[]{:S(2)}) collective-permute-start(bf16[2,16,384]{2,1,0:T(8,128)(2,1)S(1)} %get-tuple-element.11), channel_id=1, source_target_pairs={{0,20},{1,21},{2,22},{3,23},{4,16},{5,17},{6,18},{7,19},{8,28},{9,... | collective-permute-start | bytes 73736 | tf_op jit(solution)/shard_map/ppermute | solution.py:206
  159.9 5.6 %collective-permute-start.15 = (f32[16,256]{1,0:T(8,128)S(1)}, f32[16,256]{1,0:T(8,128)S(1)}, u32[]{:S(2)}, u32[]{:S(2)}) collective-permute-start(f32[16,256]{1,0:T(8,128)S(1)} %slice_bitcast_fusion.3), channel_id=1, source_target_pairs={{0,2},{1,3},{2,0},{3,1},{4,6},{5,7},{6,4},{7,5},{8,10},{9,11},{10,... | collective-permute-start | bytes 49160 | tf_op jit(solution)/shard_map/ppermute | solution.py:206
